TPU v7x, 512 devices: a 4x2x32 block of a 4x8x32 slice. The times are simulated.
512 devices in a mesh: grp: 2 (over y), tm: 64 (over z, core), space: 4 (over x).
Axes of the slice: x: 4, y: 2, z: 32, core: 2. Of those that a mesh axis runs over, the one named last changes fastest.
The devices are a block of a 4x8x32 slice.
Arguments:
- forcing: float32 [512, 32, 8, 128], P(('grp', 'tm'), 'space'), parts along dimension 0, may hold values from -6 to 6
- start_field: float32 [64, 8, 128], P(('grp', 'space')), parts along dimension 0, may hold values from -6 to 6
- velocity: float32 [3, 32, 8, 128], P(None, 'space'), may hold values from -0.5 to 0.5
- diffusivity: float32 [2], P('grp'), parts along dimension 0, may hold values from 0.3 to 1
Outputs:
- iterate: float32 [512, 32, 8, 128], P(('grp', 'tm'), 'space'), parts along dimension 0
There are 2 independent parts, one for each index of `grp`. A program takes and returns all parts, laid end to end along the dimension named above; an argument that names none is the same for every part. Nothing has to cross between parts.
All inputs are finite; a program needn't handle non-finite values.
Results may differ from a plain program's by a relative error of at most 0.0001.
Values sent between devices are 32-bit elements; how exact they have to be, the bound alone decides.
No kernel may reach another device: no remote copies, remote signals or barrier semaphores. Data moves between devices by JAX's collectives and lax.ppermute only.
A program may use at most 64 MiB of HBM per device.

v0:
```python
import jax
import jax.numpy as jnp
from jax import lax
from jax.experimental import pallas as pl
from jax.experimental.pallas import tpu as pltpu
from jax.sharding import PartitionSpec as P

SWEEPS = 4
FACTOR = 4
RUN = 2 * FACTOR
TIME_UNIT = 0.5
LEVELS = 4
VMEM = pl.BlockSpec(memory_space=pltpu.VMEM)
SMEM = pl.BlockSpec(memory_space=pltpu.SMEM)
HBM_F32 = jnp.float32


def field(*lead):
    return jax.ShapeDtypeStruct(lead + (8, 128), jnp.float32)


def phi(get, put, coef, ab, level):
    rows = coef.shape[1]
    a, b = ab[level, 0], ab[level, 1]
    v = [get(r) for r in range(rows)]
    base = None
    for sweep in range(SWEEPS):
        new = []
        for r in range(rows):
            x = v[r]
            t = coef[2, r] * pltpu.roll(x, x.shape[0] - 1, 0) + coef[3, r] * pltpu.roll(x, 1, 0)
            t = t + (coef[4, r] * pltpu.roll(x, x.shape[1] - 1, 1) + coef[5, r] * pltpu.roll(x, 1, 1))
            if r + 1 < rows:
                t = t + coef[0, r] * v[r + 1]
            if r > 0:
                t = t + coef[1, r] * v[r - 1]
            new.append(a * get(r) + b * t)
        v = new
    for r in range(rows):
        put(r, v[r])


def fill_coefficients(coef, ab, velocity_row, kappa):
    rows = coef.shape[1]
    k = jnp.full(coef.shape[2:], kappa, jnp.float32)
    for r in range(rows):
        for axis in range(3):
            half = 0.5 * velocity_row(axis, r)
            coef[2 * axis, r] = k - half
            coef[2 * axis + 1, r] = k + half
    for level in range(LEVELS):
        h = TIME_UNIT * float(FACTOR) ** level
        a = 1.0 / (1.0 + (6.0 * h) * k)
        ab[level, 0] = a
        ab[level, 1] = h * a


def place():
    count = lax.axis_size("tm")
    rank = lax.axis_index("tm")
    shifted = (rank + 1) % count
    return count // RUN, rank, shifted // RUN, shifted % RUN


def spread_kernel(kappa, gathered, send, kept, coef, ab, fields):
    runs, rank, run, member = place()
    slab = lax.axis_index("space")
    slabs, chunk = gathered.shape[:2]
    rows_slab = chunk // 8
    rows = slabs * rows_slab
    points = 4

    def row(item, r):
        return gathered[r // rows_slab, item * rows_slab + r % rows_slab]

    fill_coefficients(coef, ab, lambda axis, r: row(points + axis, r), kappa[0])
    first = (rank == 0).astype(jnp.float32)
    ZERO, FORCE, START = 0, 1, 5
    RHO = START + 8
    for r in range(rows):
        fields[ZERO, r] = jnp.zeros(fields.shape[2:], jnp.float32)
        fields[START, r] = row(points + 3, r) * first
        for i in range(points):
            fields[FORCE + i, r] = row(i, r)

    def step(src, dst, level, add):
        phi(
            lambda r: fields[src, r],
            lambda r, value: fields.__setitem__((dst, r), value + fields[add, r]),
            coef, ab, level,
        )

    Y = RHO + 7
    Z1, Z2 = Y + 1, Y + 2
    E1 = Z2 + 1
    H = E1 + 3
    power = RHO + (FACTOR - 1 - member) % FACTOR
    y = jnp.where(member < FACTOR, Y, power)
    odd = run % 2 == 0
    z = jnp.where(odd, Z2, y)

    def body(n, carry):
        main = n < 14
        m = n - 14
        src = jnp.where(m == 0, power, jnp.where(m == 1, y, jnp.where(m == 3, z, Y + m - 1)))
        pair = (m - 6) // 2
        hsrc = jnp.where(m % 2 == 0, jnp.where(pair == 0, z, E1 + pair - 1), Y + m - 1)
        src = jnp.where(m >= 6, hsrc, src)
        src = jnp.where(main, START + n, src)
        dst = jnp.where(main, START + n + 1, Y + m)
        level = jnp.where(main, jnp.where(n < 8, 0, 1), jnp.where((m >= 3) & (m < 6), 3, 2))
        add = jnp.where(n < points, FORCE + n, ZERO)
        step(src, dst, level, add)
        return carry

    lax.fori_loop(0, 26, body, 0)

    def store(target, source):
        for j in range(RUN):
            send[j, target] = fields[source, slab * rows_slab + j]

    valid = (run > 0) | (member > 0)
    this_run = run + 1
    level2 = run // 2 + 1
    for target in range(RUN):
        goal = target + 1 if target else RUN + 1
        if goal % 2 == 1:
            k = (goal + 1) // 2 - 1 - level2
            source = jnp.where(k == 0, z, E1 + k - 1)
            use = k >= 0
        else:
            k = goal // 2 - 1 - level2
            source = jnp.where(k < 0, y, H + 2 * k + 1)
            use = goal > this_run
        source = jnp.where(valid & use, source, ZERO)
        store(target, source)
    for j in range(RUN):
        source = jnp.where((j > member) & valid, RHO + jnp.maximum(j - member - 1, 0), ZERO)
        source = jnp.where(j == member, START + 4, source)
        store(RUN + j, source)
    for i in range(points - 1):
        for r in range(rows_slab):
            kept[i, r] = fields[START + 1 + i, slab * rows_slab + r]


def sum_kernel(received, targets, prefixes):
    for t in range(RUN):
        total, prefix = received[0, t], received[0, RUN + t]
        for j in range(1, received.shape[0]):
            total = total + received[j, t]
            prefix = prefix + received[j, RUN + t]
        targets[t] = total
        prefixes[t] = prefix


def share_kernel(received, prefixes, send):
    total = received[0]
    for j in range(1, received.shape[0]):
        total = total + received[j]
    for j in range(RUN):
        own = prefixes[j]
        before = prefixes[max(j - 1, 0)]
        for s in range(send.shape[1]):
            send[j, s, 0] = total
            send[j, s, 1] = own
            send[j, s, 2] = before


def boundary_kernel(received, coef, ab, after, before, v):
    runs, rank, run, member = place()
    rows = coef.shape[1]
    slabs = received.shape[1]
    rows_slab = rows // slabs
    real = jnp.where((run > 0) | (member == 0), 1.0, 0.0)

    def item(which, r):
        return received[r % rows_slab, r // rows_slab, which]

    for r in range(rows):
        v[r] = item(0, r) * real
    ones = member % FACTOR
    odd = member % 2
    twos = member // FACTOR

    def body(n, carry):
        phi(lambda r: v[r], lambda r, value: v.__setitem__(r, value), coef, ab, jnp.where(n < twos, 2, 1))
        return carry

    lax.fori_loop(0, twos + ones - odd, body, 0)
    keep = jnp.where(rank == 0, 0.0, 1.0)
    for r in range(rows):
        before[r] = (item(2, r) + v[r]) * keep
    lax.fori_loop(twos + ones - odd, twos + ones, body, 0)
    for r in range(rows):
        after[r] = item(1, r) + v[r]


def final_kernel(passed, before, after, kept, coef, ab, out, v):
    runs, rank, run, member = place()
    slab = lax.axis_index("space")
    rows = coef.shape[1]
    rows_slab = out.shape[1]
    partner = member % 2 == 0
    for r in range(rows):
        v[r] = jnp.where(partner, passed[r], before[r])
    for i in range(3):
        phi(lambda r: v[r], lambda r, value: v.__setitem__(r, value), coef, ab, 0)
        for r in range(rows_slab):
            out[i, r] = kept[i, r] + v[slab * rows_slab + r]
    for r in range(rows_slab):
        out[3, r] = after[slab * rows_slab + r]


def call(kernel, inputs, outputs, scratch=(), smem=()):
    return pl.pallas_call(
        kernel,
        out_shape=outputs,
        in_specs=[SMEM if i in smem else VMEM for i in range(len(inputs))],
        out_specs=jax.tree.map(lambda _: VMEM, outputs),
        scratch_shapes=[pltpu.VMEM(s, jnp.float32) for s in scratch],
    )(*inputs)


def local(forcing, start_field, velocity, diffusivity):
    count = lax.axis_size("tm")
    slabs = lax.axis_size("space")
    runs = count // RUN
    rows_slab = forcing.shape[1]
    rows = rows_slab * slabs
    tile = forcing.shape[2:]

    near = [[(RUN * g + j - 1) % count for j in range(RUN)] for g in range(runs)]
    far = [[(RUN * g + j - 1) % count for g in range(runs)] for j in range(RUN)]
    wide = [[q * slabs + s for q in group for s in range(slabs)] for group in near]

    own = jnp.concatenate([forcing, velocity, start_field[None]], axis=0)
    own = own.reshape((1, 8 * rows_slab) + tile)
    gathered = lax.all_to_all(
        jnp.broadcast_to(own, (slabs,) + own.shape[1:]), "space", 0, 0, tiled=True
    )
    send, kept, coef, ab = call(
        spread_kernel,
        (diffusivity, gathered),
        (field(RUN, 2 * RUN), field(3, rows_slab), field(6, rows), field(LEVELS, 2)),
        scratch=[(32, rows) + tile],
        smem=(0,),
    )
    received = lax.all_to_all(send, "tm", 0, 0, axis_index_groups=near, tiled=True)
    targets, prefixes = call(sum_kernel, (received,), (field(RUN), field(RUN)))
    received = lax.all_to_all(targets, "tm", 0, 0, axis_index_groups=far, tiled=True)
    send = call(share_kernel, (received, prefixes), field(RUN, slabs, 3))
    send = send.reshape((RUN * slabs, 3) + tile)
    received = lax.all_to_all(send, ("tm", "space"), 0, 0, axis_index_groups=wide, tiled=True)
    received = received.reshape((RUN, slabs, 3) + tile)
    after, before = call(
        boundary_kernel, (received, coef, ab), (field(rows), field(rows)), scratch=[(rows,) + tile]
    )
    passed = lax.ppermute(after, "tm", [(q, q + 1) for q in range(0, count, 2)])
    return call(
        final_kernel,
        (passed, before, after, kept, coef, ab),
        field(4, rows_slab),
        scratch=[(rows,) + tile],
    )


def solution(mesh):
    if mesh.shape["tm"] != FACTOR**3:
        raise ValueError("time axis")
    placed = (
        P(("grp", "tm"), "space", None, None),
        P(("grp", "space"), None, None),
        P(None, "space", None, None),
        P("grp"),
    )
    return jax.shard_map(
        local,
        mesh=mesh,
        in_specs=placed,
        out_specs=P(("grp", "tm"), "space", None, None),
        check_vma=False,
    )
```

profile of v0, /device:TPU:33, one launch (start us, length us, event | category | flops | bytes accessed | tf_op | source)
XLA Modules:
  0.0 160.7 jit_solution(13728988751671350835)
XLA Ops:
  0.0 1.0 pad_maximum_fusion
  1.0 1.0 broadcast_in_dim.12
  2.0 5.1 %all-to-all-start = ((f32[4,64,8,128]{3,2,1,0:T(8,128)}), f32[4,64,8,128]{3,2,1,0:T(8,128)S(1)}, u32[]{:S(2)}, u32[]{:S(2)}) async-start(f32[4,64,8,128]{3,2,1,0:T(8,128)} %broadcast_in_dim.12), calls=%async_computation | async-start | bytes 2097152 | tf_op jit(solution)/shard_map/all_to_all | solution.py:238
  7.8 9.1 %all-to-all-done.gathered = f32[4,64,8,128]{3,2,1,0:T(8,128)S(1)} async-done(((f32[4,64,8,128]{3,2,1,0:T(8,128)}), f32[4,64,8,128]{3,2,1,0:T(8,128)S(1)}, u32[]{:S(2)}, u32[]{:S(2)}) %all-to-all-start) | async-done | bytes 1048608 | tf_op jit(solution)/shard_map/all_to_all | solution.py:238
  16.9 0.0 copy-start
  16.9 1.0 copy-done
  17.9 17.0 %shard_map.46 = (f32[8,16,8,128]{3,2,1,0:T(8,128)}, f32[3,8,8,128]{3,2,1,0:T(8,128)}, f32[6,32,8,128]{3,2,1,0:T(8,128)}, f32[4,2,8,128]{3,2,1,0:T(8,128)}) custom-call(f32[1]{0:T(128)S(6)} %copy.5.kappa, f32[4,64,8,128]{3,2,1,0:T(8,128)} %copy-done), custom_call_target="tpu_custom_call" | custom-call | tf_op jit(solution)/shard_map/pallas_call | solution.py:215
  34.9 65.3 %all_to_all.20.received = f32[8,16,8,128]{3,2,1,0:T(8,128)} all-to-all(f32[8,16,8,128]{3,2,1,0:T(8,128)} %get-tuple-element.13), channel_id=1, replica_groups={{252,0,4,8,12,16,20,24},{28,32,36,40,44,48,52,56},{60,64,68,72,76,80,84..., dimensions={0} | all-to-all | bytes 1048576 | tf_op jit(solution)/shard_map/all_to_all | solution.py:248
  100.2 1.7 %shard_map.47 = (f32[8,8,128]{2,1,0:T(8,128)}, f32[8,8,128]{2,1,0:T(8,128)}) custom-call(f32[8,16,8,128]{3,2,1,0:T(8,128)} %all_to_all.20.received), custom_call_target="tpu_custom_call" | custom-call | tf_op jit(solution)/shard_map/pallas_call | solution.py:215
  101.8 27.4 %all_to_all.21.received = f32[8,8,128]{2,1,0:T(8,128)} all-to-all(f32[8,8,128]{2,1,0:T(8,128)} %get-tuple-element.14), channel_id=1, replica_groups={{252,28,60,92,124,156,188,220},{0,32,64,96,128,160,192,224},{4,36,68,10..., dimensions={0} | all-to-all | bytes 65536 | tf_op jit(solution)/shard_map/all_to_all | solution.py:250
  129.2 1.5 shard_map.48
  130.8 20.1 %all_to_all.22 = f32[32,3,8,128]{3,2,1,0:T(8,128)} all-to-all(f32[32,3,8,128]{3,2,1,0:T(8,128)} %bitcast.4), channel_id=1, replica_groups={{252,253,254,255,0,1,2,3,4,5,6,7,8,9,10,11,12,13,14,15,16,17,18,19,20,2..., dimensions={0} | all-to-all | bytes 786432 | tf_op jit(solution)/shard_map/all_to_all | solution.py:253
  150.8 2.7 %shard_map.49 = (f32[32,8,128]{2,1,0:T(8,128)}, f32[32,8,128]{2,1,0:T(8,128)}) custom-call(f32[8,4,3,8,128]{4,3,2,1,0:T(8,128)} %bitcast.5, f32[6,32,8,128]{3,2,1,0:T(8,128)} %get-tuple-element.16.coef, f32[4,2,8,128]{3,2,1,0:T(8,128)} %get-tuple-element.17.ab), custom_call_target="tpu_custom_call" | custom-call | tf_op jit(solution)/shard_map/pallas_call | solution.py:215
  153.5 1.3 collective-permute-start
  154.8 2.2 %collective-permute-done.passed = f32[32,8,128]{2,1,0:T(8,128)S(1)} collective-permute-done((f32[32,8,128]{2,1,0:T(8,128)}, f32[32,8,128]{2,1,0:T(8,128)S(1)}, u32[]{:S(2)}, u32[]{:S(2)}) %collective-permute-start) | collective-permute-done | bytes 131104 | tf_op jit(solution)/shard_map/ppermute | solution.py:258
  157.0 0.0 copy-start.1
  157.0 0.7 copy-done.1
  157.6 3.1 %shard_map.50 = f32[4,8,8,128]{3,2,1,0:T(8,128)} custom-call(f32[32,8,128]{2,1,0:T(8,128)} %copy-done.1, f32[32,8,128]{2,1,0:T(8,128)} %get-tuple-element.19.before, f32[32,8,128]{2,1,0:T(8,128)} %get-tuple-element.18.after, f32[3,8,8,128]{3,2,1,0:T(8,128)} %get-tuple-element.20.kept, f32[6,32,8,128]{3,2,1,0:T(8,128)} %get-tuple-element.16.coef, ...), custom_call_target="tpu_custom_call" | custom-call | tf_op jit(solution)/shard_map/pallas_call | solution.py:215
Async XLA Ops:
  2.0 14.9 %all-to-all-start = ((f32[4,64,8,128]{3,2,1,0:T(8,128)}), f32[4,64,8,128]{3,2,1,0:T(8,128)S(1)}, u32[]{:S(2)}, u32[]{:S(2)}) async-start(f32[4,64,8,128]{3,2,1,0:T(8,128)} %broadcast_in_dim.12), calls=%async_computation | async-start | bytes 2097152 | tf_op jit(solution)/shard_map/all_to_all | solution.py:238
  16.9 1.0 copy-start
  153.5 3.5 %collective-permute-start = (f32[32,8,128]{2,1,0:T(8,128)}, f32[32,8,128]{2,1,0:T(8,128)S(1)}, u32[]{:S(2)}, u32[]{:S(2)}) collective-permute-start(f32[32,8,128]{2,1,0:T(8,128)} %get-tuple-element.18.after), channel_id=1, source_target_pairs={{0,4},{8,12},{16,20},{24,28},{32,36},{40,44},{48,52},{56,60},{64,6... | collective-permute-start | bytes 393224 | tf_op jit(solution)/shard_map/ppermute | solution.py:258
  157.0 0.7 copy-start.1
where the time goes:
time: 161 us
  blocking collectives  113 us (70%)
  Pallas kernels  26 us (16%)
  waiting for transfers between devices  11.3 us (7%)
  starting transfers between devices  6.41 us (4%)
  local copies, waits for them, and re-layouts  2.65 us (2%)
    all_to_all x1, blocking collectives, local(): lax.all_to_all(send, 'tm', 0, 0, axis_index_groups=near, tiled=True)  65.3 us
    all_to_all x1, blocking collectives, local(): lax.all_to_all(targets, 'tm', 0, 0, axis_index_groups=far, tiled=True)  27.4 us
    pallas_call x5, Pallas kernels, call(): pl.pallas_call(kernel, out_shape=outputs, in_specs=[SMEM if i in smem els...  26 us
    all_to_all x1, blocking collectives, local(): lax.all_to_all(send, ('tm', 'space'), 0, 0, axis_index_groups=wide, tiled...  20.1 us
    all_to_all x1, waiting for transfers between devices, local(): lax.all_to_all(jnp.broadcast_to(own, (slabs,) + own.shape[1:]), 'space',...  9.09 us
    all_to_all x1, starting transfers between devices, local(): lax.all_to_all(jnp.broadcast_to(own, (slabs,) + own.shape[1:]), 'space',...  5.12 us
  transfers between devices with their start and end apart: 2, of which 2 were waited for; matrix products, arithmetic and copies ran while one was open for 0% of the time, Pallas kernels for 0%

commit v1 on v0

v1 whole, which is shorter than its diff:
```python
import jax
import jax.numpy as jnp
from jax import lax
from jax.experimental import pallas as pl
from jax.experimental.pallas import tpu as pltpu
from jax.sharding import PartitionSpec as P

SWEEPS = 4
FACTOR = 4
RUN = 2 * FACTOR
TIME_UNIT = 0.5
LEVELS = 4
VMEM = pl.BlockSpec(memory_space=pltpu.VMEM)
SMEM = pl.BlockSpec(memory_space=pltpu.SMEM)


def field(*lead):
    return jax.ShapeDtypeStruct(lead + (8, 128), jnp.float32)


def phi(get, put, coef, ab, level):
    rows = coef.shape[1]
    a, b = ab[level, 0], ab[level, 1]
    v = [get(r) for r in range(rows)]
    base = None
    for sweep in range(SWEEPS):
        new = []
        for r in range(rows):
            x = v[r]
            t = coef[2, r] * pltpu.roll(x, x.shape[0] - 1, 0) + coef[3, r] * pltpu.roll(x, 1, 0)
            t = t + (coef[4, r] * pltpu.roll(x, x.shape[1] - 1, 1) + coef[5, r] * pltpu.roll(x, 1, 1))
            if r + 1 < rows:
                t = t + coef[0, r] * v[r + 1]
            if r > 0:
                t = t + coef[1, r] * v[r - 1]
            new.append(a * get(r) + b * t)
        v = new
    for r in range(rows):
        put(r, v[r])


def fill_coefficients(coef, ab, velocity_row, kappa):
    rows = coef.shape[1]
    k = jnp.full(coef.shape[2:], kappa, jnp.float32)
    for r in range(rows):
        for axis in range(3):
            half = 0.5 * velocity_row(axis, r)
            coef[2 * axis, r] = k - half
            coef[2 * axis + 1, r] = k + half
    for level in range(LEVELS):
        h = TIME_UNIT * float(FACTOR) ** level
        a = 1.0 / (1.0 + (6.0 * h) * k)
        ab[level, 0] = a
        ab[level, 1] = h * a


def place():
    rank = lax.axis_index("tm")
    return rank // RUN, rank % RUN


def chain_kernel(kappa, gathered, last, kept, coef, ab, fields):
    slab = lax.axis_index("space")
    slabs, chunk = gathered.shape[:2]
    rows_slab = chunk // 8
    rows = slabs * rows_slab
    points = 4

    def row(item, r):
        return gathered[r // rows_slab, item * rows_slab + r % rows_slab]

    fill_coefficients(coef, ab, lambda axis, r: row(points + axis, r), kappa[0])
    first = (lax.axis_index("tm") == 0).astype(jnp.float32)
    for r in range(rows):
        fields[0, r] = row(points + 3, r) * first

    def body(n, carry):
        phi(
            lambda r: fields[n, r],
            lambda r, value: fields.__setitem__((n + 1, r), value + row(n, r)),
            coef, ab, 0,
        )
        return carry

    lax.fori_loop(0, points, body, 0)
    for r in range(rows):
        last[r] = fields[points, r]
    for i in range(points):
        for r in range(rows_slab):
            kept[i, r] = fields[1 + i, slab * rows_slab + r]


def spread_kernel(before, kept, coef, ab, send, held, fields):
    run, member = place()
    slab = lax.axis_index("space")
    rows = coef.shape[1]
    rows_slab = kept.shape[1]
    RHO = 4
    Y = RHO + 7
    Z2 = Y + 2
    E1 = Z2 + 1
    H = E1 + 3
    ZERO = fields.shape[0] - 1
    for r in range(rows):
        fields[0, r] = before[r]
    for j in range(rows_slab):
        fields[ZERO, slab * rows_slab + j] = jnp.zeros(fields.shape[2:], jnp.float32)
    power = RHO + (FACTOR - 1 - member) % FACTOR
    y = jnp.where(member < FACTOR, Y, power)
    z = jnp.where(run % 2 == 0, Z2, y)

    def body(n, carry):
        m = n - 10
        src = jnp.where(m == 0, power, jnp.where(m == 1, y, jnp.where(m == 3, z, Y + m - 1)))
        pair = (m - 6) // 2
        hsrc = jnp.where(m % 2 == 0, jnp.where(pair == 0, z, E1 + pair - 1), Y + m - 1)
        src = jnp.where(m >= 6, hsrc, src)
        src = jnp.where(m < 0, n, src)
        dst = jnp.where(m < 0, n + 1, Y + m)
        level = jnp.where(m < 0, jnp.where(n < 4, 0, 1), jnp.where((m >= 3) & (m < 6), 3, 2))
        phi(
            lambda r: fields[src, r],
            lambda r, value: fields.__setitem__((dst, r), value),
            coef, ab, level,
        )
        return carry

    lax.fori_loop(0, 22, body, 0)

    def store(slot, source):
        for j in range(RUN):
            send[j, slot] = fields[source, slab * rows_slab + j]

    level2 = run // 2 + 1
    for slot in range(RUN):
        goal = slot + 2
        if goal % 2 == 1:
            k = (goal + 1) // 2 - 1 - level2
            source = jnp.where(k == 0, z, E1 + k - 1)
            use = k >= 0
        else:
            k = goal // 2 - 1 - level2
            source = jnp.where(k < 0, y, H + 2 * k + 1)
            use = goal > run + 1
        store(slot, jnp.where(use, source, ZERO))
    for j in range(1, RUN):
        store(RUN + j - 1, jnp.where(j > member, RHO + jnp.maximum(j - member - 1, 0), ZERO))
    for r in range(rows_slab):
        for i in range(3):
            held[i, r] = kept[i, r] + fields[1 + i, slab * rows_slab + r]
        held[3, r] = kept[3, r]
        held[4, r] = fields[RHO, slab * rows_slab + r]


def sum_kernel(received, goals, prefixes):
    for t in range(2 * RUN - 1):
        total = received[0, t]
        for j in range(1, received.shape[0]):
            total = total + received[j, t]
        if t < RUN:
            goals[t] = total
        else:
            prefixes[t - RUN] = total


def share_kernel(goals, prefixes, send):
    run, _ = place()
    tile = goals.shape[1:]
    entry = jnp.where(run > 0, 1.0, 0.0) * goals[jnp.maximum(run - 1, 0)]
    leave = goals[run]
    for j in range(RUN):
        prefix = prefixes[j - 1] if j else jnp.zeros(tile, jnp.float32)
        extra = leave if j == RUN - 1 else prefixes[FACTOR - 1]
        for s in range(send.shape[1]):
            send[j, s, 0] = entry
            send[j, s, 1] = prefix
            send[j, s, 2] = extra


def final_kernel(received, held, coef, ab, out, v):
    run, member = place()
    slab = lax.axis_index("space")
    rows = coef.shape[1]
    rows_slab = out.shape[1]

    def item(which, r):
        return received[r % rows_slab, r // rows_slab, which]

    for r in range(rows):
        v[0, r] = item(0, r)
        v[1, r] = item(0, r)
    ones = member % FACTOR
    twos = member // FACTOR

    def apply(dst, src, level):
        phi(lambda r: v[src, r], lambda r, value: v.__setitem__((dst, r), value), coef, ab, level)

    def body(n, carry):
        apply(1, 1, jnp.where(n < twos, 2, 1))
        return carry

    lax.fori_loop(0, twos + ones, body, 0)
    for r in range(rows):
        v[1, r] = v[1, r] + item(1, r)
    middle = member == FACTOR - 1
    apply(2, jnp.where(middle, 0, 1), jnp.where(middle, 2, 1))
    end = member == RUN - 1
    for r in range(rows_slab):
        extra = received[r, slab, 2]
        added = jnp.where(middle, extra, held[4, r])
        moved = jnp.where(end, extra, v[2, slab * rows_slab + r] + added)
        out[3, r] = held[3, r] + moved

    def last(i, carry):
        apply(1, 1, 0)
        for r in range(rows_slab):
            out[i, r] = held[i, r] + v[1, slab * rows_slab + r]
        return carry

    lax.fori_loop(0, 3, last, 0)


def call(kernel, inputs, outputs, scratch=(), smem=(), mib=4):
    return pl.pallas_call(
        kernel,
        out_shape=outputs,
        in_specs=[SMEM if i in smem else VMEM for i in range(len(inputs))],
        out_specs=jax.tree.map(lambda _: VMEM, outputs),
        scratch_shapes=[pltpu.VMEM(s, jnp.float32) for s in scratch],
        compiler_params=pltpu.CompilerParams(vmem_limit_bytes=mib << 20),
    )(*inputs)


def local(forcing, start_field, velocity, diffusivity):
    count = lax.axis_size("tm")
    slabs = lax.axis_size("space")
    runs = count // RUN
    rows_slab = forcing.shape[1]
    rows = rows_slab * slabs
    tile = forcing.shape[2:]

    near = [[RUN * g + j for j in range(RUN)] for g in range(runs)]
    wide = [[q * slabs + s for q in group for s in range(slabs)] for group in near]

    own = jnp.concatenate([forcing, velocity, start_field[None]], axis=0)
    own = own.reshape((1, 8 * rows_slab) + tile)
    gathered = lax.all_to_all(
        jnp.broadcast_to(own, (slabs,) + own.shape[1:]), "space", 0, 0, tiled=True
    )
    last, kept, coef, ab = call(
        chain_kernel,
        (diffusivity, gathered),
        (field(rows), field(4, rows_slab), field(6, rows), field(LEVELS, 2)),
        scratch=[(5, rows) + tile],
        smem=(0,),
        mib=6,
    )
    before = lax.ppermute(last, "tm", [(q, q + 1) for q in range(count - 1)])
    send, held = call(
        spread_kernel,
        (before, kept, coef, ab),
        (field(RUN, 2 * RUN - 1), field(5, rows_slab)),
        scratch=[(25, rows) + tile],
        mib=8,
    )
    received = lax.all_to_all(send, "tm", 0, 0, axis_index_groups=near, tiled=True)
    goals, prefixes = call(sum_kernel, (received,), (field(RUN), field(RUN - 1)))
    for g in range(runs - 1):
        goals = goals + lax.ppermute(goals, "tm", list(zip(near[g], near[g + 1])))
    send = call(share_kernel, (goals, prefixes), field(RUN, slabs, 3))
    send = send.reshape((RUN * slabs, 3) + tile)
    received = lax.all_to_all(send, ("tm", "space"), 0, 0, axis_index_groups=wide, tiled=True)
    received = received.reshape((RUN, slabs, 3) + tile)
    return call(
        final_kernel,
        (received, held, coef, ab),
        field(4, rows_slab),
        scratch=[(3, rows) + tile],
    )


def solution(mesh):
    if mesh.shape["tm"] != FACTOR**3:
        raise ValueError("time axis")
    placed = (
        P(("grp", "tm"), "space", None, None),
        P(("grp", "space"), None, None),
        P(None, "space", None, None),
        P("grp"),
    )
    return jax.shard_map(
        local,
        mesh=mesh,
        in_specs=placed,
        out_specs=P(("grp", "tm"), "space", None, None),
        check_vma=False,
    )
```

time: 161 us -> 115 us (0.71)
  blocking collectives: 113 us -> 35.2 us
  waiting for transfers between devices: 11.3 us -> 42.6 us
  starting transfers between devices: 6.41 us -> 21 us
  Pallas kernels: 26 us -> 13.2 us
    all_to_all x1, blocking collectives: 65.3 us -> 16.3 us  [local(): lax.all_to_all(send, 'tm', 0, 0, axis_index_groups=near, tiled=True)]
    ppermute x1 -> x8, waiting for transfers between devices: 2.17 us -> 33.5 us  [the longest x1 32.5 us: local(): before = lax.ppermute(last, 'tm', [(q, q + 1) for q in range(count - 1)])]
    all_to_all x1 -> x0, blocking collectives: 27.4 us -> none  [local(): lax.all_to_all(targets, 'tm', 0, 0, axis_index_groups=far, tiled=True)]
    ppermute x1 -> x8, starting transfers between devices: 1.3 us -> 15.9 us  [the longest x1 10.6 us: local(): before = lax.ppermute(last, 'tm', [(q, q + 1) for q in range(count - 1)])]
    pallas_call x5, Pallas kernels: 26 us -> 13.2 us  [call(): pl.pallas_call(kernel, out_shape=outputs, in_specs=[SMEM if i in smem els...]
    unnamed x4 -> x0, local copies, waits for them, and re-layouts: 1.62 us -> none
  transfers between devices with their start and end apart: 2 -> 9, of which waited for: 2 -> 3; matrix products, arithmetic and copies ran while one was open for 0% -> 0% of each run, Pallas kernels for 0% -> 0%
where the time goes in v1:
time: 115 us
  waiting for transfers between devices  42.6 us (37%)
  blocking collectives  35.2 us (31%)
  starting transfers between devices  21 us (18%)
  Pallas kernels  13.2 us (11%)
    ppermute x1, waiting for transfers between devices, local(): before = lax.ppermute(last, 'tm', [(q, q + 1) for q in range(count - 1)])  32.5 us
    all_to_all x1, blocking collectives, local(): lax.all_to_all(send, ('tm', 'space'), 0, 0, axis_index_groups=wide, tiled...  19 us
    all_to_all x1, blocking collectives, local(): lax.all_to_all(send, 'tm', 0, 0, axis_index_groups=near, tiled=True)  16.3 us
    pallas_call x5, Pallas kernels, call(): pl.pallas_call(kernel, out_shape=outputs, in_specs=[SMEM if i in smem els...  13.2 us
    ppermute x1, starting transfers between devices, local(): before = lax.ppermute(last, 'tm', [(q, q + 1) for q in range(count - 1)])  10.6 us
    all_to_all x1, waiting for transfers between devices, local(): lax.all_to_all(jnp.broadcast_to(own, (slabs,) + own.shape[1:]), 'space',...  9.09 us
    ppermute x7, starting transfers between devices, local(): goals = goals + lax.ppermute(goals, 'tm', list(zip(near[g], near[g + 1])))  5.27 us
    all_to_all x1, starting transfers between devices, local(): lax.all_to_all(jnp.broadcast_to(own, (slabs,) + own.shape[1:]), 'space',...  5.12 us
  transfers between devices with their start and end apart: 9, of which 3 were waited for; matrix products, arithmetic and copies ran while one was open for 0% of the time, Pallas kernels for 0%

profile of v1, /device:TPU:33, one launch (start us, length us, event | category | flops | bytes accessed | tf_op | source)
XLA Modules:
  0.0 114.9 jit_solution(11709409547681105368)
XLA Ops:
  0.0 1.0 pad_maximum_fusion
  1.0 1.0 broadcast_in_dim.12
  2.0 5.1 %all-to-all-start = ((f32[4,64,8,128]{3,2,1,0:T(8,128)}), f32[4,64,8,128]{3,2,1,0:T(8,128)S(1)}, u32[]{:S(2)}, u32[]{:S(2)}) async-start(f32[4,64,8,128]{3,2,1,0:T(8,128)} %broadcast_in_dim.12), calls=%async_computation | async-start | bytes 2097152 | tf_op jit(solution)/shard_map/all_to_all | solution.py:247
  7.8 9.1 %all-to-all-done.gathered = f32[4,64,8,128]{3,2,1,0:T(8,128)S(1)} async-done(((f32[4,64,8,128]{3,2,1,0:T(8,128)}), f32[4,64,8,128]{3,2,1,0:T(8,128)S(1)}, u32[]{:S(2)}, u32[]{:S(2)}) %all-to-all-start) | async-done | bytes 1048608 | tf_op jit(solution)/shard_map/all_to_all | solution.py:247
  16.9 1.7 %shard_map.46 = (f32[32,8,128]{2,1,0:T(8,128)S(1)}, f32[4,8,8,128]{3,2,1,0:T(8,128)S(1)}, f32[6,32,8,128]{3,2,1,0:T(8,128)S(1)}, f32[4,2,8,128]{3,2,1,0:T(8,128)S(1)}) custom-call(f32[1]{0:T(128)S(6)} %copy.5.kappa, f32[4,64,8,128]{3,2,1,0:T(8,128)S(1)} %all-to-all-done.gathered), custom_call_target="tpu_custom_call" | custom-call | tf_op jit(solution)/shard_map/pallas_call | solution.py:224
  18.6 10.6 %collective-permute-start = (f32[32,8,128]{2,1,0:T(8,128)S(1)}, f32[32,8,128]{2,1,0:T(8,128)S(1)}, u32[]{:S(2)}, u32[]{:S(2)}) collective-permute-start(f32[32,8,128]{2,1,0:T(8,128)S(1)} %get-tuple-element.13), channel_id=1, source_target_pairs={{0,4},{4,8},{8,12},{12,16},{16,20},{20,24},{24,28},{28,32},{32,36}... | collective-permute-start | bytes 393224 | tf_op jit(solution)/shard_map/ppermute | solution.py:258
  29.2 32.5 %collective-permute-done.before = f32[32,8,128]{2,1,0:T(8,128)S(1)} collective-permute-done((f32[32,8,128]{2,1,0:T(8,128)S(1)}, f32[32,8,128]{2,1,0:T(8,128)S(1)}, u32[]{:S(2)}, u32[]{:S(2)}) %collective-permute-start) | collective-permute-done | bytes 131104 | tf_op jit(solution)/shard_map/ppermute | solution.py:258
  61.7 8.8 %shard_map.47 = (f32[8,15,8,128]{3,2,1,0:T(8,128)S(1)}, f32[5,8,8,128]{3,2,1,0:T(8,128)S(1)}) custom-call(f32[32,8,128]{2,1,0:T(8,128)S(1)} %collective-permute-done.before, f32[4,8,8,128]{3,2,1,0:T(8,128)S(1)} %get-tuple-element.14.kept, f32[6,32,8,128]{3,2,1,0:T(8,128)S(1)} %get-tuple-element.15.coef, f32[4,2,8,128]{3,2,1,0:T(8,128)S(1)} %get-tuple-element.16.ab), custom_call_target="tpu_custom_call" | custom-call | tf_op jit(solution)/shard_map/pallas_call | solution.py:224
  70.4 16.3 %all_to_all.15.received = f32[8,15,8,128]{3,2,1,0:T(8,128)S(1)} all-to-all(f32[8,15,8,128]{3,2,1,0:T(8,128)S(1)} %get-tuple-element.17), channel_id=1, replica_groups={{0,4,8,12,16,20,24,28},{32,36,40,44,48,52,56,60},{64,68,72,76,80,84,88,..., dimensions={0} | all-to-all | bytes 983040 | tf_op jit(solution)/shard_map/all_to_all | solution.py:266
  86.7 1.3 %collective-permute-start.1 = (f32[8,8,128]{2,1,0:T(8,128)S(1)}, f32[8,8,128]{2,1,0:T(8,128)S(1)}, u32[]{:S(2)}, u32[]{:S(2)}) collective-permute-start(f32[8,8,128]{2,1,0:T(8,128)S(1)} %get-tuple-element.18), channel_id=1, source_target_pairs={{0,32},{4,36},{8,40},{12,44},{16,48},{20,52},{24,56},{28,60},{1,33... | collective-permute-start | bytes 98312 | tf_op jit(solution)/shard_map/ppermute | solution.py:269
  88.0 1.0 collective-permute-done.1
  89.0 0.7 collective-permute-start.2
  89.7 0.0 collective-permute-done.2
  89.7 0.7 collective-permute-start.3
  90.4 0.0 collective-permute-done.3
  90.4 0.7 collective-permute-start.4
  91.1 0.0 collective-permute-done.4
  91.1 0.7 collective-permute-start.5
  91.8 0.0 collective-permute-done.5
  91.8 0.7 collective-permute-start.6
  92.5 0.0 collective-permute-done.6
  92.5 0.7 collective-permute-start.7
  93.2 19.0 %all_to_all.16 = f32[32,3,8,128]{3,2,1,0:T(8,128)S(1)} all-to-all(f32[32,3,8,128]{3,2,1,0:T(8,128)S(1)} %bitcast.4), channel_id=1, replica_groups={{0,1,2,3,4,5,6,7,8,9,10,11,12,13,14,15,16,17,18,19,20,21,22,23,24,25,26..., dimensions={0} | all-to-all | bytes 786432 | tf_op jit(solution)/shard_map/all_to_all | solution.py:272
  112.2 2.7 %shard_map.50 = f32[4,8,8,128]{3,2,1,0:T(8,128)} custom-call(f32[8,4,3,8,128]{4,3,2,1,0:T(8,128)S(1)} %bitcast.5, f32[5,8,8,128]{3,2,1,0:T(8,128)S(1)} %get-tuple-element.20.held, f32[6,32,8,128]{3,2,1,0:T(8,128)S(1)} %get-tuple-element.15.coef, f32[4,2,8,128]{3,2,1,0:T(8,128)S(1)} %get-tuple-element.16.ab), custom_call_target="tpu_custom_call" | custom-call | tf_op jit(solution)/shard_map/pallas_call | solution.py:224
  (10 shorter events, 0.1 us)
Async XLA Ops:
  2.0 14.9 %all-to-all-start = ((f32[4,64,8,128]{3,2,1,0:T(8,128)}), f32[4,64,8,128]{3,2,1,0:T(8,128)S(1)}, u32[]{:S(2)}, u32[]{:S(2)}) async-start(f32[4,64,8,128]{3,2,1,0:T(8,128)} %broadcast_in_dim.12), calls=%async_computation | async-start | bytes 2097152 | tf_op jit(solution)/shard_map/all_to_all | solution.py:247
  18.6 43.1 %collective-permute-start = (f32[32,8,128]{2,1,0:T(8,128)S(1)}, f32[32,8,128]{2,1,0:T(8,128)S(1)}, u32[]{:S(2)}, u32[]{:S(2)}) collective-permute-start(f32[32,8,128]{2,1,0:T(8,128)S(1)} %get-tuple-element.13), channel_id=1, source_target_pairs={{0,4},{4,8},{8,12},{12,16},{16,20},{20,24},{24,28},{28,32},{32,36}... | collective-permute-start | bytes 393224 | tf_op jit(solution)/shard_map/ppermute | solution.py:258
  86.7 2.3 %collective-permute-start.1 = (f32[8,8,128]{2,1,0:T(8,128)S(1)}, f32[8,8,128]{2,1,0:T(8,128)S(1)}, u32[]{:S(2)}, u32[]{:S(2)}) collective-permute-start(f32[8,8,128]{2,1,0:T(8,128)S(1)} %get-tuple-element.18), channel_id=1, source_target_pairs={{0,32},{4,36},{8,40},{12,44},{16,48},{20,52},{24,56},{28,60},{1,33... | collective-permute-start | bytes 98312 | tf_op jit(solution)/shard_map/ppermute | solution.py:269
  89.0 0.7 collective-permute-start.2
  89.7 0.7 collective-permute-start.3
  90.4 0.7 collective-permute-start.4
  91.1 0.7 collective-permute-start.5
  91.8 0.7 collective-permute-start.6
  92.5 0.7 collective-permute-start.7

commit v2 on v1

v2 whole, which is shorter than its diff:
```python
import jax
import jax.numpy as jnp
from jax import lax
from jax.experimental import pallas as pl
from jax.experimental.pallas import tpu as pltpu
from jax.sharding import PartitionSpec as P

SWEEPS = 4
FACTOR = 4
TIME_UNIT = 0.5
LEVELS = 4
VMEM = pl.BlockSpec(memory_space=pltpu.VMEM)
SMEM = pl.BlockSpec(memory_space=pltpu.SMEM)


def field(*lead):
    return jax.ShapeDtypeStruct(lead + (8, 128), jnp.float32)


def phi(get, put, coef, ab, level):
    rows = coef.shape[1]
    a, b = ab[level, 0], ab[level, 1]
    v = [get(r) for r in range(rows)]
    base = None
    for sweep in range(SWEEPS):
        new = []
        for r in range(rows):
            x = v[r]
            t = coef[2, r] * pltpu.roll(x, x.shape[0] - 1, 0) + coef[3, r] * pltpu.roll(x, 1, 0)
            t = t + (coef[4, r] * pltpu.roll(x, x.shape[1] - 1, 1) + coef[5, r] * pltpu.roll(x, 1, 1))
            if r + 1 < rows:
                t = t + coef[0, r] * v[r + 1]
            if r > 0:
                t = t + coef[1, r] * v[r - 1]
            new.append(a * get(r) + b * t)
        v = new
    for r in range(rows):
        put(r, v[r])


def fill_coefficients(coef, ab, velocity_row, kappa):
    rows = coef.shape[1]
    k = jnp.full(coef.shape[2:], kappa, jnp.float32)
    for r in range(rows):
        for axis in range(3):
            half = 0.5 * velocity_row(axis, r)
            coef[2 * axis, r] = k - half
            coef[2 * axis + 1, r] = k + half
    for level in range(LEVELS):
        h = TIME_UNIT * float(FACTOR) ** level
        a = 1.0 / (1.0 + (6.0 * h) * k)
        ab[level, 0] = a
        ab[level, 1] = h * a


def place():
    rank = lax.axis_index("tm")
    block = rank // FACTOR
    return block // FACTOR, block % FACTOR, rank % FACTOR


def chain_kernel(kappa, gathered, last, kept, coef, ab, fields):
    slab = lax.axis_index("space")
    slabs, chunk = gathered.shape[:2]
    rows_slab = chunk // 8
    rows = slabs * rows_slab
    points = 4

    def row(item, r):
        return gathered[r // rows_slab, item * rows_slab + r % rows_slab]

    fill_coefficients(coef, ab, lambda axis, r: row(points + axis, r), kappa[0])
    first = (lax.axis_index("tm") == 0).astype(jnp.float32)
    for r in range(rows):
        fields[0, r] = row(points + 3, r) * first

    def body(n, carry):
        phi(
            lambda r: fields[n, r],
            lambda r, value: fields.__setitem__((n + 1, r), value + row(n, r)),
            coef, ab, 0,
        )
        return carry

    lax.fori_loop(0, points, body, 0)
    for r in range(rows):
        last[r] = fields[points, r]
    for i in range(points):
        for r in range(rows_slab):
            kept[i, r] = fields[1 + i, slab * rows_slab + r]


def residual_kernel(before, kept, coef, ab, send, held, fields):
    slab = lax.axis_index("space")
    rows = coef.shape[1]
    rows_slab = kept.shape[1]
    for r in range(rows):
        fields[0, r] = before[r]

    def body(n, carry):
        phi(
            lambda r: fields[n, r],
            lambda r, value: fields.__setitem__((n + 1, r), value),
            coef, ab, 0,
        )
        return carry

    lax.fori_loop(0, 4, body, 0)
    for r in range(rows):
        value = fields[4, r]
        for j in range(send.shape[0]):
            send[j, r] = value
    for r in range(rows_slab):
        for i in range(3):
            held[i, r] = kept[i, r] + fields[1 + i, slab * rows_slab + r]
        held[3, r] = kept[3, r]


def spread_kernel(residuals, coef, ab, parts, prefix, added, fields):
    wide, place2, member = place()
    slab = lax.axis_index("space")
    rows = coef.shape[1]
    rows_slab = added.shape[0]
    own = parts.shape[1]
    for r in range(rows):
        fields[0, r] = jnp.zeros(fields.shape[2:], jnp.float32)
        fields[1, r] = residuals[0, r]

    def step(src, dst, level, add):
        phi(
            lambda r: fields[src, r],
            lambda r, value: fields.__setitem__((dst, r), add(r, value)),
            coef, ab, level,
        )

    def sums(n, carry):
        step(n, n + 1, 1, lambda r, value: value + residuals[n, r])
        return carry

    lax.fori_loop(1, FACTOR, sums, 0)
    total = FACTOR
    z = total + FACTOR - 1 - place2

    def powers(n, carry):
        src = jnp.where(n == 7, z, n)
        step(src, n + 1, jnp.where(n < 7, 2, 3), lambda r, value: value)
        return carry

    lax.fori_loop(4, 10, powers, 0)

    def store(slot, source):
        for j in range(own):
            parts[slot, j] = fields[source, slab * rows_slab + member * own + j]

    for later in range(1, FACTOR):
        n = later - 1 - place2
        store(later - 1, jnp.where(n >= 0, total + n, 0))
    for goal in range(FACTOR):
        n = goal - wide
        store(FACTOR - 1 + goal, jnp.where(n < 0, 0, jnp.where(n == 0, z, 7 + n)))
    for r in range(rows):
        prefix[r] = fields[member, r]
    end = member == FACTOR - 1
    for r in range(rows_slab):
        at = slab * rows_slab + r
        added[r] = jnp.where(end, fields[total, at], residuals[member, at])


def share_kernel(parts, entry, handed, send):
    wide, place2, _ = place()
    last = place2 == FACTOR - 1
    inner = jnp.where(place2 > 0, 1.0, 0.0)
    for j in range(parts.shape[1]):
        outer = jnp.where(last, entry[jnp.maximum(wide - 1, 0), j], handed[j])
        level2 = parts[jnp.maximum(place2 - 1, 0), j] * inner
        for a in range(send.shape[0]):
            for s in range(send.shape[1]):
                send[a, s, 0, j] = outer
                send[a, s, 1, j] = level2


def final_kernel(received, prefix, added, held, coef, ab, out, v):
    wide, place2, member = place()
    slab = lax.axis_index("space")
    rows = coef.shape[1]
    rows_slab = out.shape[1]
    own = received.shape[3]

    def item(which, r):
        return received[r % rows_slab // own, r // rows_slab, which, r % own]

    for r in range(rows):
        v[0, r] = item(0, r)
        v[1, r] = item(0, r)
        v[3, r] = item(1, r)

    def apply(dst, src, level):
        phi(lambda r: v[src, r], lambda r, value: v.__setitem__((dst, r), value), coef, ab, level)

    def body(level):
        def run(n, carry):
            apply(1, 1, level)
            return carry

        return run

    lax.fori_loop(0, place2, body(2), 0)
    for r in range(rows):
        entry = v[1, r] + v[3, r]
        v[1, r] = entry
        v[4, r] = entry
    lax.fori_loop(0, member, body(1), 0)
    for r in range(rows):
        v[1, r] = v[1, r] + prefix[r]
        v[5, r] = jnp.zeros(v.shape[2:], jnp.float32)
    end = member == FACTOR - 1
    both = end & (place2 == FACTOR - 1)
    apply(2, jnp.where(both, 0, jnp.where(end, 4, 1)), jnp.where(both, 3, jnp.where(end, 2, 1)))

    def second(n, carry):
        apply(5, 3, 2)
        return carry

    lax.fori_loop(0, jnp.where(both, 1, 0), second, 0)
    for r in range(rows_slab):
        at = slab * rows_slab + r
        out[3, r] = held[3, r] + (v[2, at] + v[5, at] + added[r])

    def last(i, carry):
        apply(1, 1, 0)
        for r in range(rows_slab):
            out[i, r] = held[i, r] + v[1, slab * rows_slab + r]
        return carry

    lax.fori_loop(0, 3, last, 0)


def call(kernel, inputs, outputs, scratch=(), smem=(), mib=4):
    return pl.pallas_call(
        kernel,
        out_shape=outputs,
        in_specs=[SMEM if i in smem else VMEM for i in range(len(inputs))],
        out_specs=jax.tree.map(lambda _: VMEM, outputs),
        scratch_shapes=[pltpu.VMEM(s, jnp.float32) for s in scratch],
        compiler_params=pltpu.CompilerParams(vmem_limit_bytes=mib << 20),
    )(*inputs)


def local(forcing, start_field, velocity, diffusivity):
    count = lax.axis_size("tm")
    slabs = lax.axis_size("space")
    blocks = count // FACTOR
    wides = blocks // FACTOR
    rows_slab = forcing.shape[1]
    rows = rows_slab * slabs
    own_rows = rows_slab // FACTOR
    tile = forcing.shape[2:]

    near = [[FACTOR * m + j for j in range(FACTOR)] for m in range(blocks)]
    square = [[q * slabs + s for q in group for s in range(slabs)] for group in near]

    def hop(value, pairs):
        moves = []
        for source, target in pairs:
            moves += zip(near[source[0] * FACTOR + source[1]], near[target[0] * FACTOR + target[1]])
        return lax.ppermute(value, "tm", moves)

    own = jnp.concatenate([forcing, velocity, start_field[None]], axis=0)
    own = own.reshape((1, 8 * rows_slab) + tile)
    gathered = lax.all_to_all(
        jnp.broadcast_to(own, (slabs,) + own.shape[1:]), "space", 0, 0, tiled=True
    )
    last, kept, coef, ab = call(
        chain_kernel,
        (diffusivity, gathered),
        (field(rows), field(4, rows_slab), field(6, rows), field(LEVELS, 2)),
        scratch=[(5, rows) + tile],
        smem=(0,),
        mib=6,
    )
    before = lax.ppermute(last, "tm", [(q, q + 1) for q in range(count - 1)])
    send, held = call(
        residual_kernel,
        (before, kept, coef, ab),
        (field(FACTOR, rows), field(4, rows_slab)),
        scratch=[(5, rows) + tile],
    )
    residuals = lax.all_to_all(send, "tm", 0, 0, axis_index_groups=near, tiled=True)
    parts, prefix, added = call(
        spread_kernel,
        (residuals, coef, ab),
        (field(2 * FACTOR - 1, own_rows), field(rows), field(rows_slab)),
        scratch=[(11, rows) + tile],
        mib=6,
    )
    ends = FACTOR - 1
    parts = parts + hop(parts, [((w, i), (w, i + 1)) for w in range(wides) for i in (0, 2)])
    to_last = hop(parts, [((w, 1), (w, 3)) for w in range(wides)])
    to_next = hop(parts, [((w, 1), (w, 2)) for w in range(wides)])
    parts = parts + to_last + to_next
    goals = parts[FACTOR - 1 :]
    entry = jnp.zeros_like(goals)
    for w in range(wides - 1):
        entry = entry + hop(goals + entry, [((w, ends), (w + 1, ends))])
    wide = lax.div(lax.axis_index("tm"), count // wides)
    leave = lax.dynamic_slice(goals + entry, (wide, 0, 0, 0), (1,) + goals.shape[1:])[0]
    handed = jnp.zeros_like(leave)
    for i in range(ends):
        handed = handed + hop(leave, [((w, ends), (w + 1, i)) for w in range(wides - 1)])
    send = call(share_kernel, (parts, entry, handed), field(FACTOR, slabs, 2, own_rows))
    send = send.reshape((FACTOR * slabs, 2, own_rows) + tile)
    received = lax.all_to_all(send, ("tm", "space"), 0, 0, axis_index_groups=square, tiled=True)
    received = received.reshape((FACTOR, slabs, 2, own_rows) + tile)
    return call(
        final_kernel,
        (received, prefix, added, held, coef, ab),
        field(4, rows_slab),
        scratch=[(6, rows) + tile],
    )


def solution(mesh):
    if mesh.shape["tm"] != FACTOR**3:
        raise ValueError("time axis")
    placed = (
        P(("grp", "tm"), "space", None, None),
        P(("grp", "space"), None, None),
        P(None, "space", None, None),
        P("grp"),
    )
    return jax.shard_map(
        local,
        mesh=mesh,
        in_specs=placed,
        out_specs=P(("grp", "tm"), "space", None, None),
        check_vma=False,
    )
```

time: 115 us -> 111 us (0.965)
  the two profiles are of different devices: /device:TPU:33 before, /device:TPU:425 now
where the time goes in v2:
time: 111 us
  starting transfers between devices  41.2 us (37%)
  waiting for transfers between devices  28.8 us (26%)
  blocking collectives  27.9 us (25%)
  Pallas kernels  10.2 us (9%)
    ppermute x9, starting transfers between devices, hop(): return lax.ppermute(value, 'tm', moves)  30.9 us
    all_to_all x1, blocking collectives, local(): lax.all_to_all(send, ('tm', 'space'), 0, 0, axis_index_groups=square, til...  14.9 us
    all_to_all x1, waiting for transfers between devices, local(): lax.all_to_all(jnp.broadcast_to(own, (slabs,) + own.shape[1:]), 'space',...  13.7 us
    ppermute x9, waiting for transfers between devices, hop(): return lax.ppermute(value, 'tm', moves)  13.2 us
    all_to_all x1, blocking collectives, local(): lax.all_to_all(send, 'tm', 0, 0, axis_index_groups=near, tiled=True)  13 us
    pallas_call x5, Pallas kernels, call(): pl.pallas_call(kernel, out_shape=outputs, in_specs=[SMEM if i in smem els...  10.2 us
    ppermute x1, starting transfers between devices, local(): before = lax.ppermute(last, 'tm', [(q, q + 1) for q in range(count - 1)])  6.06 us
    all_to_all x1, starting transfers between devices, local(): lax.all_to_all(jnp.broadcast_to(own, (slabs,) + own.shape[1:]), 'space',...  4.3 us
  transfers between devices with their start and end apart: 11, of which 6 were waited for; matrix products, arithmetic and copies ran while one was open for 0% of the time, Pallas kernels for 0%

profile of v2, /device:TPU:425, one launch (start us, length us, event | category | flops | bytes accessed | tf_op | source)
XLA Modules:
  0.0 111.0 jit_solution(10132070220406489349)
XLA Ops:
  0.0 1.0 pad_maximum_fusion
  1.0 1.0 broadcast_in_dim.12
  2.0 4.3 %all-to-all-start = ((f32[4,64,8,128]{3,2,1,0:T(8,128)}), f32[4,64,8,128]{3,2,1,0:T(8,128)S(1)}, u32[]{:S(2)}, u32[]{:S(2)}) async-start(f32[4,64,8,128]{3,2,1,0:T(8,128)} %broadcast_in_dim.12), calls=%async_computation | async-start | bytes 2097152 | tf_op jit(solution)/shard_map/all_to_all | solution.py:270
  7.0 13.7 %all-to-all-done.gathered = f32[4,64,8,128]{3,2,1,0:T(8,128)S(1)} async-done(((f32[4,64,8,128]{3,2,1,0:T(8,128)}), f32[4,64,8,128]{3,2,1,0:T(8,128)S(1)}, u32[]{:S(2)}, u32[]{:S(2)}) %all-to-all-start) | async-done | bytes 1048608 | tf_op jit(solution)/shard_map/all_to_all | solution.py:270
  20.6 1.6 %shard_map.46 = (f32[32,8,128]{2,1,0:T(8,128)S(1)}, f32[4,8,8,128]{3,2,1,0:T(8,128)S(1)}, f32[6,32,8,128]{3,2,1,0:T(8,128)S(1)}, f32[4,2,8,128]{3,2,1,0:T(8,128)S(1)}) custom-call(f32[1]{0:T(128)S(6)} %copy.5.kappa, f32[4,64,8,128]{3,2,1,0:T(8,128)S(1)} %all-to-all-done.gathered), custom_call_target="tpu_custom_call" | custom-call | tf_op jit(solution)/shard_map/pallas_call | solution.py:239
  22.2 6.1 %collective-permute-start = (f32[32,8,128]{2,1,0:T(8,128)S(1)}, f32[32,8,128]{2,1,0:T(8,128)S(1)}, u32[]{:S(2)}, u32[]{:S(2)}) collective-permute-start(f32[32,8,128]{2,1,0:T(8,128)S(1)} %get-tuple-element.14), channel_id=1, source_target_pairs={{0,4},{4,8},{8,12},{12,16},{16,20},{20,24},{24,28},{28,32},{32,36}... | collective-permute-start | bytes 393224 | tf_op jit(solution)/shard_map/ppermute | solution.py:281
  28.3 1.9 %collective-permute-done.before = f32[32,8,128]{2,1,0:T(8,128)S(1)} collective-permute-done((f32[32,8,128]{2,1,0:T(8,128)S(1)}, f32[32,8,128]{2,1,0:T(8,128)S(1)}, u32[]{:S(2)}, u32[]{:S(2)}) %collective-permute-start) | collective-permute-done | bytes 131104 | tf_op jit(solution)/shard_map/ppermute | solution.py:281
  30.2 1.5 %shard_map.47 = (f32[4,32,8,128]{3,2,1,0:T(8,128)S(1)}, f32[4,8,8,128]{3,2,1,0:T(8,128)S(1)}) custom-call(f32[32,8,128]{2,1,0:T(8,128)S(1)} %collective-permute-done.before, f32[4,8,8,128]{3,2,1,0:T(8,128)S(1)} %get-tuple-element.15.kept, f32[6,32,8,128]{3,2,1,0:T(8,128)S(1)} %get-tuple-element.16.coef, f32[4,2,8,128]{3,2,1,0:T(8,128)S(1)} %get-tuple-element.17.ab), custom_call_target="tpu_custom_call" | custom-call | tf_op jit(solution)/shard_map/pallas_call | solution.py:239
  31.8 13.0 %all_to_all.15.residuals = f32[4,32,8,128]{3,2,1,0:T(8,128)S(1)} all-to-all(f32[4,32,8,128]{3,2,1,0:T(8,128)S(1)} %get-tuple-element.18), channel_id=1, replica_groups={{0,4,8,12},{16,20,24,28},{32,36,40,44},{48,52,56,60},{64,68,72,76},{80,..., dimensions={0} | all-to-all | bytes 1048576 | tf_op jit(solution)/shard_map/all_to_all | solution.py:288
  44.7 3.4 %shard_map.48 = (f32[7,2,8,128]{3,2,1,0:T(8,128)S(1)}, f32[32,8,128]{2,1,0:T(8,128)S(1)}, f32[8,8,128]{2,1,0:T(8,128)S(1)}) custom-call(f32[4,32,8,128]{3,2,1,0:T(8,128)S(1)} %all_to_all.15.residuals, f32[6,32,8,128]{3,2,1,0:T(8,128)S(1)} %get-tuple-element.16.coef, f32[4,2,8,128]{3,2,1,0:T(8,128)S(1)} %get-tuple-element.17.ab), custom_call_target="tpu_custom_call" | custom-call | tf_op jit(solution)/shard_map/pallas_call | solution.py:239
  48.1 1.3 %collective-permute-start.1 = (f32[7,2,8,128]{3,2,1,0:T(8,128)S(1)}, f32[7,2,8,128]{3,2,1,0:T(8,128)S(1)}, u32[]{:S(2)}, u32[]{:S(2)}) collective-permute-start(f32[7,2,8,128]{3,2,1,0:T(8,128)S(1)} %get-tuple-element.19), channel_id=1, source_target_pairs={{0,16},{4,20},{8,24},{12,28},{32,48},{36,52},{40,56},{44,60},{64,8... | collective-permute-start | bytes 172040 | tf_op jit(solution)/shard_map/ppermute | solution.py:266
  49.4 4.6 %collective-permute-done.1 = f32[7,2,8,128]{3,2,1,0:T(8,128)S(1)} collective-permute-done((f32[7,2,8,128]{3,2,1,0:T(8,128)S(1)}, f32[7,2,8,128]{3,2,1,0:T(8,128)S(1)}, u32[]{:S(2)}, u32[]{:S(2)}) %collective-permute-start.1) | collective-permute-done | bytes 57376 | tf_op jit(solution)/shard_map/ppermute | solution.py:266
  54.0 1.3 %collective-permute-start.2 = (f32[7,2,8,128]{3,2,1,0:T(8,128)S(1)}, f32[7,2,8,128]{3,2,1,0:T(8,128)S(1)}, u32[]{:S(2)}, u32[]{:S(2)}) collective-permute-start(f32[7,2,8,128]{3,2,1,0:T(8,128)S(1)} %add.33), channel_id=1, source_target_pairs={{16,48},{20,52},{24,56},{28,60},{80,112},{84,116},{88,120},{92,124... | collective-permute-start | bytes 172040 | tf_op jit(solution)/shard_map/ppermute | solution.py:266
  55.3 0.7 collective-permute-start.3
  56.0 6.9 %collective-permute-done.2 = f32[7,2,8,128]{3,2,1,0:T(8,128)S(1)} collective-permute-done((f32[7,2,8,128]{3,2,1,0:T(8,128)S(1)}, f32[7,2,8,128]{3,2,1,0:T(8,128)S(1)}, u32[]{:S(2)}, u32[]{:S(2)}) %collective-permute-start.2) | collective-permute-done | bytes 57376 | tf_op jit(solution)/shard_map/ppermute | solution.py:266
  62.9 22.3 %collective-permute-start.4 = (f32[4,2,8,128]{3,2,1,0:T(8,128)S(1)}, f32[4,2,8,128]{3,2,1,0:T(8,128)S(1)}, u32[]{:S(2)}, u32[]{:S(2)}) collective-permute-start(f32[4,2,8,128]{3,2,1,0:T(8,128)S(1)} %slice.4), channel_id=1, source_target_pairs={{48,112},{52,116},{56,120},{60,124},{49,113},{53,117},{57,121},{61... | collective-permute-start | bytes 98312 | tf_op jit(solution)/shard_map/ppermute | solution.py:266
  85.2 1.0 collective-permute-done.4
  86.9 0.7 collective-permute-start.6
  87.7 1.3 %collective-permute-start.7 = (f32[2,8,128]{2,1,0:T(8,128)S(1)}, f32[2,8,128]{2,1,0:T(8,128)S(1)}, u32[]{:S(2)}, u32[]{:S(2)}) collective-permute-start(f32[2,8,128]{2,1,0:T(8,128)S(1)} %fusion), channel_id=1, source_target_pairs={{48,64},{52,68},{56,72},{60,76},{112,128},{116,132},{120,136},{124... | collective-permute-start | bytes 24584 | tf_op jit(solution)/shard_map/ppermute | solution.py:266
  89.0 1.3 %collective-permute-start.8 = (f32[2,8,128]{2,1,0:T(8,128)S(1)}, f32[2,8,128]{2,1,0:T(8,128)S(1)}, u32[]{:S(2)}, u32[]{:S(2)}) collective-permute-start(f32[2,8,128]{2,1,0:T(8,128)S(1)} %fusion), channel_id=1, source_target_pairs={{48,80},{52,84},{56,88},{60,92},{112,144},{116,148},{120,152},{124... | collective-permute-start | bytes 24584 | tf_op jit(solution)/shard_map/ppermute | solution.py:266
  90.3 1.3 %collective-permute-start.9 = (f32[2,8,128]{2,1,0:T(8,128)S(1)}, f32[2,8,128]{2,1,0:T(8,128)S(1)}, u32[]{:S(2)}, u32[]{:S(2)}) collective-permute-start(f32[2,8,128]{2,1,0:T(8,128)S(1)} %fusion), channel_id=1, source_target_pairs={{48,96},{52,100},{56,104},{60,108},{112,160},{116,164},{120,168},{... | collective-permute-start | bytes 24584 | tf_op jit(solution)/shard_map/ppermute | solution.py:266
  91.6 0.8 collective-permute-done.9
  92.4 14.9 %all_to_all.16 = f32[16,2,2,8,128]{4,3,2,1,0:T(8,128)S(1)} all-to-all(f32[16,2,2,8,128]{4,3,2,1,0:T(8,128)S(1)} %bitcast.6), channel_id=1, replica_groups={{0,1,2,3,4,5,6,7,8,9,10,11,12,13,14,15},{16,17,18,19,20,21,22,23,24,25,..., dimensions={0} | all-to-all | bytes 524288 | tf_op jit(solution)/shard_map/all_to_all | solution.py:312
  107.3 3.7 %shard_map.50 = f32[4,8,8,128]{3,2,1,0:T(8,128)} custom-call(f32[4,4,2,2,8,128]{5,4,3,2,1,0:T(8,128)S(1)} %bitcast.7, f32[32,8,128]{2,1,0:T(8,128)S(1)} %get-tuple-element.20.prefix, f32[8,8,128]{2,1,0:T(8,128)S(1)} %get-tuple-element.21.added, f32[4,8,8,128]{3,2,1,0:T(8,128)S(1)} %get-tuple-element.22.held, f32[6,32,8,128]{3,2,1,0:T(8,128)S(1)} %get-tuple-element.16.coef, ...), custom_call_target="tpu_custom_call" | custom-call | tf_op jit(solution)/shard_map/pallas_call | solution.py:239
  (15 shorter events, 0.8 us)
Async XLA Ops:
  2.0 18.6 %all-to-all-start = ((f32[4,64,8,128]{3,2,1,0:T(8,128)}), f32[4,64,8,128]{3,2,1,0:T(8,128)S(1)}, u32[]{:S(2)}, u32[]{:S(2)}) async-start(f32[4,64,8,128]{3,2,1,0:T(8,128)} %broadcast_in_dim.12), calls=%async_computation | async-start | bytes 2097152 | tf_op jit(solution)/shard_map/all_to_all | solution.py:270
  22.2 8.0 %collective-permute-start = (f32[32,8,128]{2,1,0:T(8,128)S(1)}, f32[32,8,128]{2,1,0:T(8,128)S(1)}, u32[]{:S(2)}, u32[]{:S(2)}) collective-permute-start(f32[32,8,128]{2,1,0:T(8,128)S(1)} %get-tuple-element.14), channel_id=1, source_target_pairs={{0,4},{4,8},{8,12},{12,16},{16,20},{20,24},{24,28},{28,32},{32,36}... | collective-permute-start | bytes 393224 | tf_op jit(solution)/shard_map/ppermute | solution.py:281
  48.1 5.9 %collective-permute-start.1 = (f32[7,2,8,128]{3,2,1,0:T(8,128)S(1)}, f32[7,2,8,128]{3,2,1,0:T(8,128)S(1)}, u32[]{:S(2)}, u32[]{:S(2)}) collective-permute-start(f32[7,2,8,128]{3,2,1,0:T(8,128)S(1)} %get-tuple-element.19), channel_id=1, source_target_pairs={{0,16},{4,20},{8,24},{12,28},{32,48},{36,52},{40,56},{44,60},{64,8... | collective-permute-start | bytes 172040 | tf_op jit(solution)/shard_map/ppermute | solution.py:266
  54.0 8.9 %collective-permute-start.2 = (f32[7,2,8,128]{3,2,1,0:T(8,128)S(1)}, f32[7,2,8,128]{3,2,1,0:T(8,128)S(1)}, u32[]{:S(2)}, u32[]{:S(2)}) collective-permute-start(f32[7,2,8,128]{3,2,1,0:T(8,128)S(1)} %add.33), channel_id=1, source_target_pairs={{16,48},{20,52},{24,56},{28,60},{80,112},{84,116},{88,120},{92,124... | collective-permute-start | bytes 172040 | tf_op jit(solution)/shard_map/ppermute | solution.py:266
  55.3 7.5 %collective-permute-start.3 = (f32[7,2,8,128]{3,2,1,0:T(8,128)S(1)}, f32[7,2,8,128]{3,2,1,0:T(8,128)S(1)}, u32[]{:S(2)}, u32[]{:S(2)}) collective-permute-start(f32[7,2,8,128]{3,2,1,0:T(8,128)S(1)} %add.33), channel_id=1, source_target_pairs={{16,32},{20,36},{24,40},{28,44},{80,96},{84,100},{88,104},{92,108}... | collective-permute-start | bytes 172040 | tf_op jit(solution)/shard_map/ppermute | solution.py:266
  62.9 23.4 %collective-permute-start.4 = (f32[4,2,8,128]{3,2,1,0:T(8,128)S(1)}, f32[4,2,8,128]{3,2,1,0:T(8,128)S(1)}, u32[]{:S(2)}, u32[]{:S(2)}) collective-permute-start(f32[4,2,8,128]{3,2,1,0:T(8,128)S(1)} %slice.4), channel_id=1, source_target_pairs={{48,112},{52,116},{56,120},{60,124},{49,113},{53,117},{57,121},{61... | collective-permute-start | bytes 98312 | tf_op jit(solution)/shard_map/ppermute | solution.py:266
  86.2 0.7 collective-permute-start.5
  86.9 0.7 collective-permute-start.6
  87.7 3.9 %collective-permute-start.7 = (f32[2,8,128]{2,1,0:T(8,128)S(1)}, f32[2,8,128]{2,1,0:T(8,128)S(1)}, u32[]{:S(2)}, u32[]{:S(2)}) collective-permute-start(f32[2,8,128]{2,1,0:T(8,128)S(1)} %fusion), channel_id=1, source_target_pairs={{48,64},{52,68},{56,72},{60,76},{112,128},{116,132},{120,136},{124... | collective-permute-start | bytes 24584 | tf_op jit(solution)/shard_map/ppermute | solution.py:266
  89.0 2.6 %collective-permute-start.8 = (f32[2,8,128]{2,1,0:T(8,128)S(1)}, f32[2,8,128]{2,1,0:T(8,128)S(1)}, u32[]{:S(2)}, u32[]{:S(2)}) collective-permute-start(f32[2,8,128]{2,1,0:T(8,128)S(1)} %fusion), channel_id=1, source_target_pairs={{48,80},{52,84},{56,88},{60,92},{112,144},{116,148},{120,152},{124... | collective-permute-start | bytes 24584 | tf_op jit(solution)/shard_map/ppermute | solution.py:266
  90.3 2.1 %collective-permute-start.9 = (f32[2,8,128]{2,1,0:T(8,128)S(1)}, f32[2,8,128]{2,1,0:T(8,128)S(1)}, u32[]{:S(2)}, u32[]{:S(2)}) collective-permute-start(f32[2,8,128]{2,1,0:T(8,128)S(1)} %fusion), channel_id=1, source_target_pairs={{48,96},{52,100},{56,104},{60,108},{112,160},{116,164},{120,168},{... | collective-permute-start | bytes 24584 | tf_op jit(solution)/shard_map/ppermute | solution.py:266

commit v3 on v2

--- a/solution.py
+++ b/solution.py
@@ -59,6 +59,20 @@
     return block // FACTOR, block % FACTOR, rank % FACTOR
 
 
+def lay_out_kernel(forcing, velocity, start, own, done):
+    copies = []
+    for s in range(own.shape[0]):
+        copies += [
+            pltpu.make_async_copy(forcing, own.at[s, pl.ds(0, 4)], done.at[s, 0]),
+            pltpu.make_async_copy(velocity, own.at[s, pl.ds(4, 3)], done.at[s, 1]),
+            pltpu.make_async_copy(start, own.at[s, 7], done.at[s, 2]),
+        ]
+    for copy in copies:
+        copy.start()
+    for copy in copies:
+        copy.wait()
+
+
 def chain_kernel(kappa, gathered, last, kept, coef, ab, fields):
     slab = lax.axis_index("space")
     slabs, chunk = gathered.shape[:2]
@@ -265,11 +279,16 @@
             moves += zip(near[source[0] * FACTOR + source[1]], near[target[0] * FACTOR + target[1]])
         return lax.ppermute(value, "tm", moves)
 
-    own = jnp.concatenate([forcing, velocity, start_field[None]], axis=0)
-    own = own.reshape((1, 8 * rows_slab) + tile)
-    gathered = lax.all_to_all(
-        jnp.broadcast_to(own, (slabs,) + own.shape[1:]), "space", 0, 0, tiled=True
-    )
+    own = pl.pallas_call(
+        lay_out_kernel,
+        out_shape=field(slabs, 8, rows_slab),
+        in_specs=[pl.BlockSpec(memory_space=pltpu.HBM)] * 3,
+        out_specs=pl.BlockSpec(memory_space=pltpu.HBM),
+        scratch_shapes=[pltpu.SemaphoreType.DMA((slabs, 3))],
+        compiler_params=pltpu.CompilerParams(vmem_limit_bytes=60 << 20),
+    )(forcing, velocity, start_field)
+    gathered = lax.all_to_all(own, "space", 0, 0, tiled=True)
+    gathered = gathered.reshape((slabs, 8 * rows_slab) + tile)
     last, kept, coef, ab = call(
         chain_kernel,
         (diffusivity, gathered),
@@ -294,10 +313,11 @@
         mib=6,
     )
     ends = FACTOR - 1
-    parts = parts + hop(parts, [((w, i), (w, i + 1)) for w in range(wides) for i in (0, 2)])
-    to_last = hop(parts, [((w, 1), (w, 3)) for w in range(wides)])
-    to_next = hop(parts, [((w, 1), (w, 2)) for w in range(wides)])
-    parts = parts + to_last + to_next
+    third = hop(parts, [((w, 2), (w, 3)) for w in range(wides)])
+    pair = parts + hop(parts, [((w, 0), (w, 1)) for w in range(wides)])
+    to_last = hop(pair, [((w, 1), (w, 3)) for w in range(wides)])
+    to_next = hop(pair, [((w, 1), (w, 2)) for w in range(wides)])
+    parts = pair + third + to_last + to_next
     goals = parts[FACTOR - 1 :]
     entry = jnp.zeros_like(goals)
     for w in range(wides - 1):

time: 111 us -> 138 us (1.24)
  Pallas kernels: 10.2 us -> 43.2 us
  waiting for transfers between devices: 28.8 us -> 24.2 us
    pallas_call x0 -> x1, Pallas kernels: none -> 33 us  [local(): pl.pallas_call(lay_out_kernel, out_shape=field(slabs, 8, rows_slab), in_s...]
    ppermute x9 -> x10, waiting for transfers between devices: 13.2 us -> 8.67 us  [hop(): return lax.ppermute(value, 'tm', moves)]
    ppermute x9 -> x10, starting transfers between devices: 30.9 us -> 31.5 us  [hop(): return lax.ppermute(value, 'tm', moves)]
  transfers between devices with their start and end apart: 11 -> 12, of which waited for: 6 -> 6; matrix products, arithmetic and copies ran while one was open for 0% -> 0% of each run, Pallas kernels for 0% -> 0%
where the time goes in v3:
time: 138 us
  Pallas kernels  43.2 us (31%)
  starting transfers between devices  41.9 us (30%)
  blocking collectives  27.3 us (20%)
  waiting for transfers between devices  24.2 us (18%)
    pallas_call x1, Pallas kernels, local(): pl.pallas_call(lay_out_kernel, out_shape=field(slabs, 8, rows_slab), in_s...  33 us
    ppermute x10, starting transfers between devices, hop(): return lax.ppermute(value, 'tm', moves)  31.5 us
    all_to_all x1, blocking collectives, local(): lax.all_to_all(send, ('tm', 'space'), 0, 0, axis_index_groups=square, til...  14.3 us
    all_to_all x1, waiting for transfers between devices, local(): gathered = lax.all_to_all(own, 'space', 0, 0, tiled=True)  13.7 us
    all_to_all x1, blocking collectives, local(): lax.all_to_all(send, 'tm', 0, 0, axis_index_groups=near, tiled=True)  13 us
    pallas_call x5, Pallas kernels, call(): pl.pallas_call(kernel, out_shape=outputs, in_specs=[SMEM if i in smem els...  10.2 us
    ppermute x10, waiting for transfers between devices, hop(): return lax.ppermute(value, 'tm', moves)  8.67 us
    ppermute x1, starting transfers between devices, local(): before = lax.ppermute(last, 'tm', [(q, q + 1) for q in range(count - 1)])  6.06 us
  transfers between devices with their start and end apart: 12, of which 6 were waited for; matrix products, arithmetic and copies ran while one was open for 0% of the time, Pallas kernels for 0%

profile of v3, /device:TPU:425, one launch (start us, length us, event | category | flops | bytes accessed | tf_op | source)
XLA Modules:
  0.0 137.5 jit_solution(13488092373939776706)
XLA Ops:
  0.0 33.0 %shard_map.46 = f32[4,8,8,8,128]{4,3,2,1,0:T(8,128)} custom-call(f32[4,8,8,128]{3,2,1,0:T(8,128)} %forcing.1, f32[3,8,8,128]{3,2,1,0:T(8,128)} %velocity.1, f32[8,8,128]{2,1,0:T(8,128)} %start.1), custom_call_target="tpu_custom_call" | custom-call | tf_op jit(solution)/shard_map/pallas_call | solution.py:282
  33.0 4.3 %all-to-all-start = ((f32[4,8,8,8,128]{4,3,2,1,0:T(8,128)}), f32[4,8,8,8,128]{4,3,2,1,0:T(8,128)S(1)}, u32[]{:S(2)}, u32[]{:S(2)}) async-start(f32[4,8,8,8,128]{4,3,2,1,0:T(8,128)} %shard_map.46), calls=%async_computation | async-start | bytes 2097152 | tf_op jit(solution)/shard_map/all_to_all | solution.py:290
  37.9 13.7 %all-to-all-done = f32[4,8,8,8,128]{4,3,2,1,0:T(8,128)S(1)} async-done(((f32[4,8,8,8,128]{4,3,2,1,0:T(8,128)}), f32[4,8,8,8,128]{4,3,2,1,0:T(8,128)S(1)}, u32[]{:S(2)}, u32[]{:S(2)}) %all-to-all-start) | async-done | bytes 1048608 | tf_op jit(solution)/shard_map/all_to_all | solution.py:290
  51.6 1.6 %shard_map.47 = (f32[32,8,128]{2,1,0:T(8,128)S(1)}, f32[4,8,8,128]{3,2,1,0:T(8,128)S(1)}, f32[6,32,8,128]{3,2,1,0:T(8,128)S(1)}, f32[4,2,8,128]{3,2,1,0:T(8,128)S(1)}) custom-call(f32[1]{0:T(128)S(6)} %copy.5.kappa, f32[4,64,8,128]{3,2,1,0:T(8,128)S(1)} %bitcast.5), custom_call_target="tpu_custom_call" | custom-call | tf_op jit(solution)/shard_map/pallas_call | solution.py:253
  53.2 6.1 %collective-permute-start = (f32[32,8,128]{2,1,0:T(8,128)S(1)}, f32[32,8,128]{2,1,0:T(8,128)S(1)}, u32[]{:S(2)}, u32[]{:S(2)}) collective-permute-start(f32[32,8,128]{2,1,0:T(8,128)S(1)} %get-tuple-element.14), channel_id=1, source_target_pairs={{0,4},{4,8},{8,12},{12,16},{16,20},{20,24},{24,28},{28,32},{32,36}... | collective-permute-start | bytes 393224 | tf_op jit(solution)/shard_map/ppermute | solution.py:300
  59.2 1.9 %collective-permute-done.before = f32[32,8,128]{2,1,0:T(8,128)S(1)} collective-permute-done((f32[32,8,128]{2,1,0:T(8,128)S(1)}, f32[32,8,128]{2,1,0:T(8,128)S(1)}, u32[]{:S(2)}, u32[]{:S(2)}) %collective-permute-start) | collective-permute-done | bytes 131104 | tf_op jit(solution)/shard_map/ppermute | solution.py:300
  61.2 1.5 %shard_map.48 = (f32[4,32,8,128]{3,2,1,0:T(8,128)S(1)}, f32[4,8,8,128]{3,2,1,0:T(8,128)S(1)}) custom-call(f32[32,8,128]{2,1,0:T(8,128)S(1)} %collective-permute-done.before, f32[4,8,8,128]{3,2,1,0:T(8,128)S(1)} %get-tuple-element.15.kept, f32[6,32,8,128]{3,2,1,0:T(8,128)S(1)} %get-tuple-element.16.coef, f32[4,2,8,128]{3,2,1,0:T(8,128)S(1)} %get-tuple-element.17.ab), custom_call_target="tpu_custom_call" | custom-call | tf_op jit(solution)/shard_map/pallas_call | solution.py:253
  62.7 13.0 %all_to_all.15.residuals = f32[4,32,8,128]{3,2,1,0:T(8,128)S(1)} all-to-all(f32[4,32,8,128]{3,2,1,0:T(8,128)S(1)} %get-tuple-element.18), channel_id=1, replica_groups={{0,4,8,12},{16,20,24,28},{32,36,40,44},{48,52,56,60},{64,68,72,76},{80,..., dimensions={0} | all-to-all | bytes 1048576 | tf_op jit(solution)/shard_map/all_to_all | solution.py:307
  75.7 3.4 %shard_map.49 = (f32[7,2,8,128]{3,2,1,0:T(8,128)S(1)}, f32[32,8,128]{2,1,0:T(8,128)S(1)}, f32[8,8,128]{2,1,0:T(8,128)S(1)}) custom-call(f32[4,32,8,128]{3,2,1,0:T(8,128)S(1)} %all_to_all.15.residuals, f32[6,32,8,128]{3,2,1,0:T(8,128)S(1)} %get-tuple-element.16.coef, f32[4,2,8,128]{3,2,1,0:T(8,128)S(1)} %get-tuple-element.17.ab), custom_call_target="tpu_custom_call" | custom-call | tf_op jit(solution)/shard_map/pallas_call | solution.py:253
  79.0 0.7 collective-permute-start.1
  79.7 1.3 collective-permute-start.2
  81.1 1.3 collective-permute-start.3
  82.4 0.7 collective-permute-start.4
  83.1 2.5 %collective-permute-done.2 = f32[7,2,8,128]{3,2,1,0:T(8,128)S(1)} collective-permute-done((f32[7,2,8,128]{3,2,1,0:T(8,128)S(1)}, f32[7,2,8,128]{3,2,1,0:T(8,128)S(1)}, u32[]{:S(2)}, u32[]{:S(2)}) %collective-permute-start.2) | collective-permute-done | bytes 57376 | tf_op jit(solution)/shard_map/ppermute | solution.py:280
  85.6 4.4 %collective-permute-done.3 = f32[7,2,8,128]{3,2,1,0:T(8,128)S(1)} collective-permute-done((f32[7,2,8,128]{3,2,1,0:T(8,128)S(1)}, f32[7,2,8,128]{3,2,1,0:T(8,128)S(1)}, u32[]{:S(2)}, u32[]{:S(2)}) %collective-permute-start.3) | collective-permute-done | bytes 57376 | tf_op jit(solution)/shard_map/ppermute | solution.py:280
  90.0 22.3 %collective-permute-start.5 = (f32[4,2,8,128]{3,2,1,0:T(8,128)S(1)}, f32[4,2,8,128]{3,2,1,0:T(8,128)S(1)}, u32[]{:S(2)}, u32[]{:S(2)}) collective-permute-start(f32[4,2,8,128]{3,2,1,0:T(8,128)S(1)} %slice.4), channel_id=1, source_target_pairs={{48,112},{52,116},{56,120},{60,124},{49,113},{53,117},{57,121},{61... | collective-permute-start | bytes 98312 | tf_op jit(solution)/shard_map/ppermute | solution.py:280
  112.3 1.0 collective-permute-done.5
  114.0 0.7 collective-permute-start.7
  114.8 1.3 collective-permute-start.10
  116.1 1.3 collective-permute-start.8
  117.4 1.3 collective-permute-start.9
  118.7 0.8 collective-permute-done.9
  119.5 14.3 %all_to_all.16 = f32[16,2,2,8,128]{4,3,2,1,0:T(8,128)S(1)} all-to-all(f32[16,2,2,8,128]{4,3,2,1,0:T(8,128)S(1)} %bitcast.6), channel_id=1, replica_groups={{0,1,2,3,4,5,6,7,8,9,10,11,12,13,14,15},{16,17,18,19,20,21,22,23,24,25,..., dimensions={0} | all-to-all | bytes 524288 | tf_op jit(solution)/shard_map/all_to_all | solution.py:332
  133.8 3.7 %shard_map.51 = f32[4,8,8,128]{3,2,1,0:T(8,128)} custom-call(f32[4,4,2,2,8,128]{5,4,3,2,1,0:T(8,128)S(1)} %bitcast.7, f32[32,8,128]{2,1,0:T(8,128)S(1)} %get-tuple-element.20.prefix, f32[8,8,128]{2,1,0:T(8,128)S(1)} %get-tuple-element.21.added, f32[4,8,8,128]{3,2,1,0:T(8,128)S(1)} %get-tuple-element.22.held, f32[6,32,8,128]{3,2,1,0:T(8,128)S(1)} %get-tuple-element.16.coef, ...), custom_call_target="tpu_custom_call" | custom-call | tf_op jit(solution)/shard_map/pallas_call | solution.py:253
  (16 shorter events, 0.8 us)
Async XLA Ops:
  33.0 18.6 %all-to-all-start = ((f32[4,8,8,8,128]{4,3,2,1,0:T(8,128)}), f32[4,8,8,8,128]{4,3,2,1,0:T(8,128)S(1)}, u32[]{:S(2)}, u32[]{:S(2)}) async-start(f32[4,8,8,8,128]{4,3,2,1,0:T(8,128)} %shard_map.46), calls=%async_computation | async-start | bytes 2097152 | tf_op jit(solution)/shard_map/all_to_all | solution.py:290
  53.2 8.0 %collective-permute-start = (f32[32,8,128]{2,1,0:T(8,128)S(1)}, f32[32,8,128]{2,1,0:T(8,128)S(1)}, u32[]{:S(2)}, u32[]{:S(2)}) collective-permute-start(f32[32,8,128]{2,1,0:T(8,128)S(1)} %get-tuple-element.14), channel_id=1, source_target_pairs={{0,4},{4,8},{8,12},{12,16},{16,20},{20,24},{24,28},{28,32},{32,36}... | collective-permute-start | bytes 393224 | tf_op jit(solution)/shard_map/ppermute | solution.py:300
  79.0 2.0 %collective-permute-start.1 = (f32[7,2,8,128]{3,2,1,0:T(8,128)S(1)}, f32[7,2,8,128]{3,2,1,0:T(8,128)S(1)}, u32[]{:S(2)}, u32[]{:S(2)}) collective-permute-start(f32[7,2,8,128]{3,2,1,0:T(8,128)S(1)} %get-tuple-element.19), channel_id=1, source_target_pairs={{0,16},{4,20},{8,24},{12,28},{64,80},{68,84},{72,88},{76,92},{128,... | collective-permute-start | bytes 172040 | tf_op jit(solution)/shard_map/ppermute | solution.py:280
  79.7 5.9 %collective-permute-start.2 = (f32[7,2,8,128]{3,2,1,0:T(8,128)S(1)}, f32[7,2,8,128]{3,2,1,0:T(8,128)S(1)}, u32[]{:S(2)}, u32[]{:S(2)}) collective-permute-start(f32[7,2,8,128]{3,2,1,0:T(8,128)S(1)} %get-tuple-element.19), channel_id=1, source_target_pairs={{32,48},{36,52},{40,56},{44,60},{96,112},{100,116},{104,120},{108,... | collective-permute-start | bytes 172040 | tf_op jit(solution)/shard_map/ppermute | solution.py:280
  81.1 8.9 %collective-permute-start.3 = (f32[7,2,8,128]{3,2,1,0:T(8,128)S(1)}, f32[7,2,8,128]{3,2,1,0:T(8,128)S(1)}, u32[]{:S(2)}, u32[]{:S(2)}) collective-permute-start(f32[7,2,8,128]{3,2,1,0:T(8,128)S(1)} %add.36), channel_id=1, source_target_pairs={{16,48},{20,52},{24,56},{28,60},{80,112},{84,116},{88,120},{92,124... | collective-permute-start | bytes 172040 | tf_op jit(solution)/shard_map/ppermute | solution.py:280
  82.4 7.6 %collective-permute-start.4 = (f32[7,2,8,128]{3,2,1,0:T(8,128)S(1)}, f32[7,2,8,128]{3,2,1,0:T(8,128)S(1)}, u32[]{:S(2)}, u32[]{:S(2)}) collective-permute-start(f32[7,2,8,128]{3,2,1,0:T(8,128)S(1)} %add.36), channel_id=1, source_target_pairs={{16,32},{20,36},{24,40},{28,44},{80,96},{84,100},{88,104},{92,108}... | collective-permute-start | bytes 172040 | tf_op jit(solution)/shard_map/ppermute | solution.py:280
  90.0 23.4 %collective-permute-start.5 = (f32[4,2,8,128]{3,2,1,0:T(8,128)S(1)}, f32[4,2,8,128]{3,2,1,0:T(8,128)S(1)}, u32[]{:S(2)}, u32[]{:S(2)}) collective-permute-start(f32[4,2,8,128]{3,2,1,0:T(8,128)S(1)} %slice.4), channel_id=1, source_target_pairs={{48,112},{52,116},{56,120},{60,124},{49,113},{53,117},{57,121},{61... | collective-permute-start | bytes 98312 | tf_op jit(solution)/shard_map/ppermute | solution.py:280
  113.3 0.7 collective-permute-start.6
  114.0 0.7 collective-permute-start.7
  114.8 3.9 %collective-permute-start.10 = (f32[2,8,128]{2,1,0:T(8,128)S(1)}, f32[2,8,128]{2,1,0:T(8,128)S(1)}, u32[]{:S(2)}, u32[]{:S(2)}) collective-permute-start(f32[2,8,128]{2,1,0:T(8,128)S(1)} %fusion), channel_id=1, source_target_pairs={{48,96},{52,100},{56,104},{60,108},{112,160},{116,164},{120,168},{... | collective-permute-start | bytes 24584 | tf_op jit(solution)/shard_map/ppermute | solution.py:280
  116.1 2.6 %collective-permute-start.8 = (f32[2,8,128]{2,1,0:T(8,128)S(1)}, f32[2,8,128]{2,1,0:T(8,128)S(1)}, u32[]{:S(2)}, u32[]{:S(2)}) collective-permute-start(f32[2,8,128]{2,1,0:T(8,128)S(1)} %fusion), channel_id=1, source_target_pairs={{48,64},{52,68},{56,72},{60,76},{112,128},{116,132},{120,136},{124... | collective-permute-start | bytes 24584 | tf_op jit(solution)/shard_map/ppermute | solution.py:280
  117.4 2.1 %collective-permute-start.9 = (f32[2,8,128]{2,1,0:T(8,128)S(1)}, f32[2,8,128]{2,1,0:T(8,128)S(1)}, u32[]{:S(2)}, u32[]{:S(2)}) collective-permute-start(f32[2,8,128]{2,1,0:T(8,128)S(1)} %fusion), channel_id=1, source_target_pairs={{48,80},{52,84},{56,88},{60,92},{112,144},{116,148},{120,152},{124... | collective-permute-start | bytes 24584 | tf_op jit(solution)/shard_map/ppermute | solution.py:280

commit v4 on v2

--- a/solution.py
+++ b/solution.py
@@ -294,19 +294,24 @@
         mib=6,
     )
     ends = FACTOR - 1
-    parts = parts + hop(parts, [((w, i), (w, i + 1)) for w in range(wides) for i in (0, 2)])
-    to_last = hop(parts, [((w, 1), (w, 3)) for w in range(wides)])
-    to_next = hop(parts, [((w, 1), (w, 2)) for w in range(wides)])
-    parts = parts + to_last + to_next
+    third = hop(parts, [((w, 2), (w, 3)) for w in range(wides)])
+    pair = parts + hop(parts, [((w, 0), (w, 1)) for w in range(wides)])
+    to_last = hop(pair, [((w, 1), (w, 3)) for w in range(wides)])
+    to_next = hop(pair, [((w, 1), (w, 2)) for w in range(wides)])
+    parts = pair + third + to_last + to_next
     goals = parts[FACTOR - 1 :]
-    entry = jnp.zeros_like(goals)
-    for w in range(wides - 1):
+    first = hop(goals, [((0, ends), (1, 0))])
+    entry = hop(first, [((1, 0), (1, ends))])
+    for w in range(1, wides - 1):
         entry = entry + hop(goals + entry, [((w, ends), (w + 1, ends))])
     wide = lax.div(lax.axis_index("tm"), count // wides)
     leave = lax.dynamic_slice(goals + entry, (wide, 0, 0, 0), (1,) + goals.shape[1:])[0]
-    handed = jnp.zeros_like(leave)
+    in_first = (wide == 1) & (lax.rem(lax.div(lax.axis_index("tm"), FACTOR), FACTOR) == 0)
+    leave = jnp.where(in_first, first[0], leave)
+    handed = jnp.where(in_first, first[0], 0.0)
     for i in range(ends):
-        handed = handed + hop(leave, [((w, ends), (w + 1, i)) for w in range(wides - 1)])
+        pairs = [((w, ends), (w + 1, i)) for w in range(1, wides - 1)]
+        handed = handed + hop(leave, pairs + ([((1, 0), (1, i))] if i else []))
     send = call(share_kernel, (parts, entry, handed), field(FACTOR, slabs, 2, own_rows))
     send = send.reshape((FACTOR * slabs, 2, own_rows) + tile)
     received = lax.all_to_all(send, ("tm", "space"), 0, 0, axis_index_groups=square, tiled=True)

time: 111 us -> 102 us (0.919)
  the two profiles are of different devices: /device:TPU:425 before, /device:TPU:33 now
where the time goes in v4:
time: 102 us; the launch traced here: 100 us
  waiting for transfers between devices  42.2 us (41%)
  starting transfers between devices  23.7 us (23%)
  blocking collectives  22.2 us (22%)
  Pallas kernels  9.12 us (9%)
  other arithmetic  1.07 us (1%)
  local copies, waits for them, and re-layouts  1.06 us (1%)
    ppermute x1, waiting for transfers between devices, local(): before = lax.ppermute(last, 'tm', [(q, q + 1) for q in range(count - 1)])  32.5 us
    all_to_all x1, blocking collectives, local(): lax.all_to_all(send, ('tm', 'space'), 0, 0, axis_index_groups=square, til...  11.8 us
    ppermute x1, starting transfers between devices, local(): before = lax.ppermute(last, 'tm', [(q, q + 1) for q in range(count - 1)])  10.6 us
    all_to_all x1, blocking collectives, local(): lax.all_to_all(send, 'tm', 0, 0, axis_index_groups=near, tiled=True)  10.4 us
    pallas_call x5, Pallas kernels, call(): pl.pallas_call(kernel, out_shape=outputs, in_specs=[SMEM if i in smem els...  9.12 us
    all_to_all x1, waiting for transfers between devices, local(): lax.all_to_all(jnp.broadcast_to(own, (slabs,) + own.shape[1:]), 'space',...  9.09 us
    ppermute x11, starting transfers between devices, hop(): return lax.ppermute(value, 'tm', moves)  7.93 us
    all_to_all x1, starting transfers between devices, local(): lax.all_to_all(jnp.broadcast_to(own, (slabs,) + own.shape[1:]), 'space',...  5.12 us
  transfers between devices with their start and end apart: 13, of which 3 were waited for; matrix products, arithmetic and copies ran while one was open for 0% of the time, Pallas kernels for 0%

profile of v4, /device:TPU:33, one launch (start us, length us, event | category | flops | bytes accessed | tf_op | source)
XLA Modules:
  0.0 100.2 jit_solution(9854523557825308975)
XLA Ops:
  0.0 1.0 pad_maximum_fusion
  1.0 1.1 %broadcast_in_dim.16 = f32[4,64,8,128]{3,2,1,0:T(8,128)} broadcast(f32[64,8,128]{2,1,0:T(8,128)S(1)} %bitcast.14), dimensions={1,2,3} | broadcast | bytes 1310720 | tf_op jit(solution)/shard_map/broadcast_in_dim | solution.py:271
  2.0 5.1 %all-to-all-start = ((f32[4,64,8,128]{3,2,1,0:T(8,128)}), f32[4,64,8,128]{3,2,1,0:T(8,128)S(1)}, u32[]{:S(2)}, u32[]{:S(2)}) async-start(f32[4,64,8,128]{3,2,1,0:T(8,128)} %broadcast_in_dim.16), calls=%async_computation | async-start | bytes 2097152 | tf_op jit(solution)/shard_map/all_to_all | solution.py:270
  7.8 9.1 %all-to-all-done.gathered = f32[4,64,8,128]{3,2,1,0:T(8,128)S(1)} async-done(((f32[4,64,8,128]{3,2,1,0:T(8,128)}), f32[4,64,8,128]{3,2,1,0:T(8,128)S(1)}, u32[]{:S(2)}, u32[]{:S(2)}) %all-to-all-start) | async-done | bytes 1048608 | tf_op jit(solution)/shard_map/all_to_all | solution.py:270
  16.9 1.6 %shard_map.46 = (f32[32,8,128]{2,1,0:T(8,128)S(1)}, f32[4,8,8,128]{3,2,1,0:T(8,128)S(1)}, f32[6,32,8,128]{3,2,1,0:T(8,128)S(1)}, f32[4,2,8,128]{3,2,1,0:T(8,128)S(1)}) custom-call(f32[1]{0:T(128)S(6)} %copy.5.kappa, f32[4,64,8,128]{3,2,1,0:T(8,128)S(1)} %all-to-all-done.gathered), custom_call_target="tpu_custom_call" | custom-call | tf_op jit(solution)/shard_map/pallas_call | solution.py:239
  18.5 10.6 %collective-permute-start = (f32[32,8,128]{2,1,0:T(8,128)S(1)}, f32[32,8,128]{2,1,0:T(8,128)S(1)}, u32[]{:S(2)}, u32[]{:S(2)}) collective-permute-start(f32[32,8,128]{2,1,0:T(8,128)S(1)} %get-tuple-element.14), channel_id=1, source_target_pairs={{0,4},{4,8},{8,12},{12,16},{16,20},{20,24},{24,28},{28,32},{32,36}... | collective-permute-start | bytes 393224 | tf_op jit(solution)/shard_map/ppermute | solution.py:281
  29.1 32.5 %collective-permute-done.before = f32[32,8,128]{2,1,0:T(8,128)S(1)} collective-permute-done((f32[32,8,128]{2,1,0:T(8,128)S(1)}, f32[32,8,128]{2,1,0:T(8,128)S(1)}, u32[]{:S(2)}, u32[]{:S(2)}) %collective-permute-start) | collective-permute-done | bytes 131104 | tf_op jit(solution)/shard_map/ppermute | solution.py:281
  61.6 1.5 %shard_map.47 = (f32[4,32,8,128]{3,2,1,0:T(8,128)S(1)}, f32[4,8,8,128]{3,2,1,0:T(8,128)S(1)}) custom-call(f32[32,8,128]{2,1,0:T(8,128)S(1)} %collective-permute-done.before, f32[4,8,8,128]{3,2,1,0:T(8,128)S(1)} %get-tuple-element.15.kept, f32[6,32,8,128]{3,2,1,0:T(8,128)S(1)} %get-tuple-element.16.coef, f32[4,2,8,128]{3,2,1,0:T(8,128)S(1)} %get-tuple-element.17.ab), custom_call_target="tpu_custom_call" | custom-call | tf_op jit(solution)/shard_map/pallas_call | solution.py:239
  63.1 10.4 %all_to_all.15.residuals = f32[4,32,8,128]{3,2,1,0:T(8,128)S(1)} all-to-all(f32[4,32,8,128]{3,2,1,0:T(8,128)S(1)} %get-tuple-element.18), channel_id=1, replica_groups={{0,4,8,12},{16,20,24,28},{32,36,40,44},{48,52,56,60},{64,68,72,76},{80,..., dimensions={0} | all-to-all | bytes 1048576 | tf_op jit(solution)/shard_map/all_to_all | solution.py:288
  73.5 3.4 %shard_map.48 = (f32[7,2,8,128]{3,2,1,0:T(8,128)S(1)}, f32[32,8,128]{2,1,0:T(8,128)S(1)}, f32[8,8,128]{2,1,0:T(8,128)S(1)}) custom-call(f32[4,32,8,128]{3,2,1,0:T(8,128)S(1)} %all_to_all.15.residuals, f32[6,32,8,128]{3,2,1,0:T(8,128)S(1)} %get-tuple-element.16.coef, f32[4,2,8,128]{3,2,1,0:T(8,128)S(1)} %get-tuple-element.17.ab), custom_call_target="tpu_custom_call" | custom-call | tf_op jit(solution)/shard_map/pallas_call | solution.py:239
  76.9 1.3 %collective-permute-start.1 = (f32[7,2,8,128]{3,2,1,0:T(8,128)S(1)}, f32[7,2,8,128]{3,2,1,0:T(8,128)S(1)}, u32[]{:S(2)}, u32[]{:S(2)}) collective-permute-start(f32[7,2,8,128]{3,2,1,0:T(8,128)S(1)} %get-tuple-element.19), channel_id=1, source_target_pairs={{0,16},{4,20},{8,24},{12,28},{64,80},{68,84},{72,88},{76,92},{128,... | collective-permute-start | bytes 172040 | tf_op jit(solution)/shard_map/ppermute | solution.py:266
  78.2 0.7 collective-permute-start.2
  78.9 0.6 collective-permute-done.1
  79.4 0.7 collective-permute-start.3
  80.1 0.7 collective-permute-start.4
  80.8 0.7 collective-permute-start.5
  81.5 0.7 collective-permute-start.6
  82.2 0.7 collective-permute-start.7
  82.9 0.7 collective-permute-start.8
  83.7 0.7 collective-permute-start.10
  84.3 0.7 collective-permute-start.11
  85.0 0.7 collective-permute-start.9
  85.8 11.8 %all_to_all.16 = f32[16,2,2,8,128]{4,3,2,1,0:T(8,128)S(1)} all-to-all(f32[16,2,2,8,128]{4,3,2,1,0:T(8,128)S(1)} %bitcast.12), channel_id=1, replica_groups={{0,1,2,3,4,5,6,7,8,9,10,11,12,13,14,15},{16,17,18,19,20,21,22,23,24,25,..., dimensions={0} | all-to-all | bytes 524288 | tf_op jit(solution)/shard_map/all_to_all | solution.py:317
  97.6 2.6 %shard_map.50 = f32[4,8,8,128]{3,2,1,0:T(8,128)} custom-call(f32[4,4,2,2,8,128]{5,4,3,2,1,0:T(8,128)S(1)} %bitcast.13, f32[32,8,128]{2,1,0:T(8,128)S(1)} %get-tuple-element.20.prefix, f32[8,8,128]{2,1,0:T(8,128)S(1)} %get-tuple-element.21.added, f32[4,8,8,128]{3,2,1,0:T(8,128)S(1)} %get-tuple-element.22.held, f32[6,32,8,128]{3,2,1,0:T(8,128)S(1)} %get-tuple-element.16.coef, ...), custom_call_target="tpu_custom_call" | custom-call | tf_op jit(solution)/shard_map/pallas_call | solution.py:239
  (19 shorter events, 0.2 us)
Async XLA Ops:
  2.0 14.9 %all-to-all-start = ((f32[4,64,8,128]{3,2,1,0:T(8,128)}), f32[4,64,8,128]{3,2,1,0:T(8,128)S(1)}, u32[]{:S(2)}, u32[]{:S(2)}) async-start(f32[4,64,8,128]{3,2,1,0:T(8,128)} %broadcast_in_dim.16), calls=%async_computation | async-start | bytes 2097152 | tf_op jit(solution)/shard_map/all_to_all | solution.py:270
  18.5 43.1 %collective-permute-start = (f32[32,8,128]{2,1,0:T(8,128)S(1)}, f32[32,8,128]{2,1,0:T(8,128)S(1)}, u32[]{:S(2)}, u32[]{:S(2)}) collective-permute-start(f32[32,8,128]{2,1,0:T(8,128)S(1)} %get-tuple-element.14), channel_id=1, source_target_pairs={{0,4},{4,8},{8,12},{12,16},{16,20},{20,24},{24,28},{28,32},{32,36}... | collective-permute-start | bytes 393224 | tf_op jit(solution)/shard_map/ppermute | solution.py:281
  76.9 2.5 %collective-permute-start.1 = (f32[7,2,8,128]{3,2,1,0:T(8,128)S(1)}, f32[7,2,8,128]{3,2,1,0:T(8,128)S(1)}, u32[]{:S(2)}, u32[]{:S(2)}) collective-permute-start(f32[7,2,8,128]{3,2,1,0:T(8,128)S(1)} %get-tuple-element.19), channel_id=1, source_target_pairs={{0,16},{4,20},{8,24},{12,28},{64,80},{68,84},{72,88},{76,92},{128,... | collective-permute-start | bytes 172040 | tf_op jit(solution)/shard_map/ppermute | solution.py:266
  78.2 2.6 %collective-permute-start.2 = (f32[7,2,8,128]{3,2,1,0:T(8,128)S(1)}, f32[7,2,8,128]{3,2,1,0:T(8,128)S(1)}, u32[]{:S(2)}, u32[]{:S(2)}) collective-permute-start(f32[7,2,8,128]{3,2,1,0:T(8,128)S(1)} %get-tuple-element.19), channel_id=1, source_target_pairs={{32,48},{36,52},{40,56},{44,60},{96,112},{100,116},{104,120},{108,... | collective-permute-start | bytes 172040 | tf_op jit(solution)/shard_map/ppermute | solution.py:266
  79.4 1.3 %collective-permute-start.3 = (f32[7,2,8,128]{3,2,1,0:T(8,128)S(1)}, f32[7,2,8,128]{3,2,1,0:T(8,128)S(1)}, u32[]{:S(2)}, u32[]{:S(2)}) collective-permute-start(f32[7,2,8,128]{3,2,1,0:T(8,128)S(1)} %add.39), channel_id=1, source_target_pairs={{16,48},{20,52},{24,56},{28,60},{80,112},{84,116},{88,120},{92,124... | collective-permute-start | bytes 172040 | tf_op jit(solution)/shard_map/ppermute | solution.py:266
  80.1 0.7 collective-permute-start.4
  80.8 0.7 collective-permute-start.5
  81.5 0.7 collective-permute-start.6
  82.2 0.7 collective-permute-start.7
  82.9 0.7 collective-permute-start.8
  83.7 2.0 %collective-permute-start.10 = (f32[2,8,128]{2,1,0:T(8,128)S(1)}, f32[2,8,128]{2,1,0:T(8,128)S(1)}, u32[]{:S(2)}, u32[]{:S(2)}) collective-permute-start(f32[2,8,128]{2,1,0:T(8,128)S(1)} %fusion.1), channel_id=1, source_target_pairs={{112,144},{116,148},{120,152},{124,156},{176,208},{180,212},{184,2... | collective-permute-start | bytes 24584 | tf_op jit(solution)/shard_map/ppermute | solution.py:266
  84.3 1.4 %collective-permute-start.11 = (f32[2,8,128]{2,1,0:T(8,128)S(1)}, f32[2,8,128]{2,1,0:T(8,128)S(1)}, u32[]{:S(2)}, u32[]{:S(2)}) collective-permute-start(f32[2,8,128]{2,1,0:T(8,128)S(1)} %fusion.1), channel_id=1, source_target_pairs={{112,160},{116,164},{120,168},{124,172},{176,224},{180,228},{184,2... | collective-permute-start | bytes 24584 | tf_op jit(solution)/shard_map/ppermute | solution.py:266
  85.0 0.7 collective-permute-start.9

commit v5 on v4

--- a/solution.py
+++ b/solution.py
@@ -90,7 +90,7 @@
             kept[i, r] = fields[1 + i, slab * rows_slab + r]
 
 
-def residual_kernel(before, kept, coef, ab, send, held, fields):
+def residual_kernel(before, kept, coef, ab, residual, held, fields):
     slab = lax.axis_index("space")
     rows = coef.shape[1]
     rows_slab = kept.shape[1]
@@ -107,9 +107,7 @@
 
     lax.fori_loop(0, 4, body, 0)
     for r in range(rows):
-        value = fields[4, r]
-        for j in range(send.shape[0]):
-            send[j, r] = value
+        residual[r] = fields[4, r]
     for r in range(rows_slab):
         for i in range(3):
             held[i, r] = kept[i, r] + fields[1 + i, slab * rows_slab + r]
@@ -166,12 +164,11 @@
         added[r] = jnp.where(end, fields[total, at], residuals[member, at])
 
 
-def share_kernel(parts, entry, handed, send):
-    wide, place2, _ = place()
-    last = place2 == FACTOR - 1
+def share_kernel(parts, entry, send):
+    _, place2, _ = place()
     inner = jnp.where(place2 > 0, 1.0, 0.0)
     for j in range(parts.shape[1]):
-        outer = jnp.where(last, entry[jnp.maximum(wide - 1, 0), j], handed[j])
+        outer = entry[j]
         level2 = parts[jnp.maximum(place2 - 1, 0), j] * inner
         for a in range(send.shape[0]):
             for s in range(send.shape[1]):
@@ -279,13 +276,13 @@
         mib=6,
     )
     before = lax.ppermute(last, "tm", [(q, q + 1) for q in range(count - 1)])
-    send, held = call(
+    residual, held = call(
         residual_kernel,
         (before, kept, coef, ab),
-        (field(FACTOR, rows), field(4, rows_slab)),
+        (field(rows), field(4, rows_slab)),
         scratch=[(5, rows) + tile],
     )
-    residuals = lax.all_to_all(send, "tm", 0, 0, axis_index_groups=near, tiled=True)
+    residuals = lax.all_gather(residual, "tm", axis_index_groups=near)
     parts, prefix, added = call(
         spread_kernel,
         (residuals, coef, ab),
@@ -301,18 +298,25 @@
     parts = pair + third + to_last + to_next
     goals = parts[FACTOR - 1 :]
     first = hop(goals, [((0, ends), (1, 0))])
-    entry = hop(first, [((1, 0), (1, ends))])
-    for w in range(1, wides - 1):
-        entry = entry + hop(goals + entry, [((w, ends), (w + 1, ends))])
-    wide = lax.div(lax.axis_index("tm"), count // wides)
-    leave = lax.dynamic_slice(goals + entry, (wide, 0, 0, 0), (1,) + goals.shape[1:])[0]
-    in_first = (wide == 1) & (lax.rem(lax.div(lax.axis_index("tm"), FACTOR), FACTOR) == 0)
-    leave = jnp.where(in_first, first[0], leave)
-    handed = jnp.where(in_first, first[0], 0.0)
-    for i in range(ends):
-        pairs = [((w, ends), (w + 1, i)) for w in range(1, wides - 1)]
-        handed = handed + hop(leave, pairs + ([((1, 0), (1, i))] if i else []))
-    send = call(share_kernel, (parts, entry, handed), field(FACTOR, slabs, 2, own_rows))
+    rank = lax.axis_index("tm")
+    wide = lax.div(rank, count // wides)
+
+    def carry_on(goals, first):
+        entry = hop(first, [((1, 0), (1, ends))])
+        for w in range(1, wides - 1):
+            entry = entry + hop(goals + entry, [((w, ends), (w + 1, ends))])
+        leave = lax.dynamic_slice(goals + entry, (wide, 0, 0, 0), (1,) + goals.shape[1:])[0]
+        in_first = (wide == 1) & (lax.rem(lax.div(rank, FACTOR), FACTOR) == 0)
+        leave = jnp.where(in_first, first[0], leave)
+        handed = jnp.where(in_first, first[0], 0.0)
+        for i in range(ends):
+            pairs = [((w, ends), (w + 1, i)) for w in range(1, wides - 1)]
+            handed = handed + hop(leave, pairs + ([((1, 0), (1, i))] if i else []))
+        last = lax.dynamic_slice(entry, (wide - 1, 0, 0, 0), (1,) + goals.shape[1:])[0]
+        return jnp.where(lax.rem(lax.div(rank, FACTOR), FACTOR) == ends, last, handed)
+
+    entry = lax.cond(wide > 0, carry_on, lambda goals, first: jnp.zeros_like(goals[0]), goals, first)
+    send = call(share_kernel, (parts, entry), field(FACTOR, slabs, 2, own_rows))
     send = send.reshape((FACTOR * slabs, 2, own_rows) + tile)
     received = lax.all_to_all(send, ("tm", "space"), 0, 0, axis_index_groups=square, tiled=True)
     received = received.reshape((FACTOR, slabs, 2, own_rows) + tile)

time: 102 us -> 100 us (0.980)
  the two profiles are of different devices: /device:TPU:33 before, /device:TPU:545 now
where the time goes in v5:
time: 100 us; the launch traced here: 99.7 us
  waiting for transfers between devices  36.4 us (36%)
  starting transfers between devices  27.7 us (28%)
  blocking collectives  23.5 us (24%)
  Pallas kernels  9.08 us (9%)
  other arithmetic  1.06 us (1%)
  local copies, waits for them, and re-layouts  1.05 us (1%)
    ppermute x11, waiting for transfers between devices, hop(): return lax.ppermute(value, 'tm', moves)  20.8 us
    ppermute x11, starting transfers between devices, hop(): return lax.ppermute(value, 'tm', moves)  17.4 us
    all_to_all x1, blocking collectives, local(): lax.all_to_all(send, ('tm', 'space'), 0, 0, axis_index_groups=square, til...  15 us
    all_to_all x1, waiting for transfers between devices, local(): lax.all_to_all(jnp.broadcast_to(own, (slabs,) + own.shape[1:]), 'space',...  13.7 us
    pallas_call x5, Pallas kernels, call(): pl.pallas_call(kernel, out_shape=outputs, in_specs=[SMEM if i in smem els...  9.08 us
    all_gather x1, blocking collectives, local(): residuals = lax.all_gather(residual, 'tm', axis_index_groups=near)  8.45 us
    ppermute x1, starting transfers between devices, local(): before = lax.ppermute(last, 'tm', [(q, q + 1) for q in range(count - 1)])  6.06 us
    all_to_all x1, starting transfers between devices, local(): lax.all_to_all(jnp.broadcast_to(own, (slabs,) + own.shape[1:]), 'space',...  4.3 us
  transfers between devices with their start and end apart: 13, of which 6 were waited for; matrix products, arithmetic and copies ran while one was open for 0% of the time, Pallas kernels for 0%

profile of v5, /device:TPU:545, one launch (start us, length us, event | category | flops | bytes accessed | tf_op | source)
XLA Modules:
  0.0 99.7 jit_solution(915628108068030255)
XLA Ops:
  0.0 1.0 pad_maximum_fusion
  1.0 1.0 %broadcast_in_dim.16 = f32[4,64,8,128]{3,2,1,0:T(8,128)} broadcast(f32[64,8,128]{2,1,0:T(8,128)S(1)} %bitcast.20), dimensions={1,2,3} | broadcast | bytes 1310720 | tf_op jit(solution)/shard_map/broadcast_in_dim | solution.py:268
  2.0 4.3 %all-to-all-start = ((f32[4,64,8,128]{3,2,1,0:T(8,128)}), f32[4,64,8,128]{3,2,1,0:T(8,128)S(1)}, u32[]{:S(2)}, u32[]{:S(2)}) async-start(f32[4,64,8,128]{3,2,1,0:T(8,128)} %broadcast_in_dim.16), calls=%async_computation | async-start | bytes 2097152 | tf_op jit(solution)/shard_map/all_to_all | solution.py:267
  7.0 13.7 %all-to-all-done.gathered = f32[4,64,8,128]{3,2,1,0:T(8,128)S(1)} async-done(((f32[4,64,8,128]{3,2,1,0:T(8,128)}), f32[4,64,8,128]{3,2,1,0:T(8,128)S(1)}, u32[]{:S(2)}, u32[]{:S(2)}) %all-to-all-start) | async-done | bytes 1048608 | tf_op jit(solution)/shard_map/all_to_all | solution.py:267
  20.6 1.6 %shard_map.46 = (f32[32,8,128]{2,1,0:T(8,128)S(1)}, f32[4,8,8,128]{3,2,1,0:T(8,128)S(1)}, f32[6,32,8,128]{3,2,1,0:T(8,128)S(1)}, f32[4,2,8,128]{3,2,1,0:T(8,128)S(1)}) custom-call(f32[1]{0:T(128)S(6)} %copy.7.kappa, f32[4,64,8,128]{3,2,1,0:T(8,128)S(1)} %all-to-all-done.gathered), custom_call_target="tpu_custom_call" | custom-call | tf_op jit(solution)/shard_map/pallas_call | solution.py:236
  22.2 6.1 %collective-permute-start.6 = (f32[32,8,128]{2,1,0:T(8,128)S(1)}, f32[32,8,128]{2,1,0:T(8,128)S(1)}, u32[]{:S(2)}, u32[]{:S(2)}) collective-permute-start(f32[32,8,128]{2,1,0:T(8,128)S(1)} %get-tuple-element.29), channel_id=1, source_target_pairs={{0,4},{4,8},{8,12},{12,16},{16,20},{20,24},{24,28},{28,32},{32,36}... | collective-permute-start | bytes 393224 | tf_op jit(solution)/shard_map/ppermute | solution.py:278
  28.3 1.9 %collective-permute-done.6.before = f32[32,8,128]{2,1,0:T(8,128)S(1)} collective-permute-done((f32[32,8,128]{2,1,0:T(8,128)S(1)}, f32[32,8,128]{2,1,0:T(8,128)S(1)}, u32[]{:S(2)}, u32[]{:S(2)}) %collective-permute-start.6) | collective-permute-done | bytes 131104 | tf_op jit(solution)/shard_map/ppermute | solution.py:278
  30.2 1.5 %shard_map.47 = (f32[32,8,128]{2,1,0:T(8,128)S(1)}, f32[4,8,8,128]{3,2,1,0:T(8,128)S(1)}) custom-call(f32[32,8,128]{2,1,0:T(8,128)S(1)} %collective-permute-done.6.before, f32[4,8,8,128]{3,2,1,0:T(8,128)S(1)} %get-tuple-element.30.kept, f32[6,32,8,128]{3,2,1,0:T(8,128)S(1)} %get-tuple-element.31.coef, f32[4,2,8,128]{3,2,1,0:T(8,128)S(1)} %get-tuple-element.32.ab), custom_call_target="tpu_custom_call" | custom-call | tf_op jit(solution)/shard_map/pallas_call | solution.py:236
  31.7 8.5 %all-gather = f32[128,8,128]{2,1,0:T(8,128)S(1)} all-gather(f32[32,8,128]{2,1,0:T(8,128)S(1)} %get-tuple-element.33), channel_id=2, replica_groups={{0,4,8,12},{16,20,24,28},{32,36,40,44},{48,52,56,60},{64,68,72,76},{80,..., dimensions={0}, use_global_device_ids=true | all-gather | bytes 655360 | tf_op jit(solution)/shard_map/all_gather | solution.py:285
  40.2 3.4 %shard_map.48 = (f32[7,2,8,128]{3,2,1,0:T(8,128)S(1)}, f32[32,8,128]{2,1,0:T(8,128)S(1)}, f32[8,8,128]{2,1,0:T(8,128)S(1)}) custom-call(f32[4,32,8,128]{3,2,1,0:T(8,128)S(1)} %bitcast.17, f32[6,32,8,128]{3,2,1,0:T(8,128)S(1)} %get-tuple-element.31.coef, f32[4,2,8,128]{3,2,1,0:T(8,128)S(1)} %get-tuple-element.32.ab), custom_call_target="tpu_custom_call" | custom-call | tf_op jit(solution)/shard_map/pallas_call | solution.py:236
  43.6 7.9 %collective-permute-start.7 = (f32[7,2,8,128]{3,2,1,0:T(8,128)S(1)}, f32[7,2,8,128]{3,2,1,0:T(8,128)S(1)}, u32[]{:S(2)}, u32[]{:S(2)}) collective-permute-start(f32[7,2,8,128]{3,2,1,0:T(8,128)S(1)} %get-tuple-element.34), channel_id=1, source_target_pairs={{0,16},{4,20},{8,24},{12,28},{64,80},{68,84},{72,88},{76,92},{128,... | collective-permute-start | bytes 172040 | tf_op jit(solution)/shard_map/ppermute | solution.py:263
  51.4 0.7 collective-permute-start.8
  53.3 0.7 collective-permute-start.9
  54.1 1.3 %collective-permute-start.11 = (f32[4,2,8,128]{3,2,1,0:T(8,128)S(1)}, f32[4,2,8,128]{3,2,1,0:T(8,128)S(1)}, u32[]{:S(2)}, u32[]{:S(2)}) collective-permute-start(f32[4,2,8,128]{3,2,1,0:T(8,128)S(1)} %slice.8), channel_id=1, source_target_pairs={{48,64},{52,68},{56,72},{60,76},{49,65},{53,69},{57,73},{61,77},{5... | collective-permute-start | bytes 98312 | tf_op jit(solution)/shard_map/ppermute | solution.py:263
  55.4 18.5 %collective-permute-done.11 = f32[4,2,8,128]{3,2,1,0:T(8,128)S(1)} collective-permute-done((f32[4,2,8,128]{3,2,1,0:T(8,128)S(1)}, f32[4,2,8,128]{3,2,1,0:T(8,128)S(1)}, u32[]{:S(2)}, u32[]{:S(2)}) %collective-permute-start.11) | collective-permute-done | bytes 32800 | tf_op jit(solution)/shard_map/ppermute | solution.py:263
  73.9 8.2 %conditional.1 = (f32[2,8,128]{2,1,0:T(8,128)S(1)}) conditional(s32[]{:T(128)} %convert_element_type.3, () %tuple.11, (s32[]{:T(128)}, f32[4,2,8,128]{3,2,1,0:T(8,128)S(1)}, f32[4,2,8,128]{3,2,1,0:T(8,128)S(1)}, s32[]{:T(128)}) %tuple.12), branch_computations={%region_0.0_spmd, %region_1.2_spmd} | conditional | flops 47127 | bytes 934383 | solution.py:318
  73.9 1.6 %collective-permute-start = (f32[4,2,8,128]{3,2,1,0:T(8,128)S(1)}, f32[4,2,8,128]{3,2,1,0:T(8,128)S(1)}, u32[]{:S(2)}, u32[]{:S(2)}) collective-permute-start(f32[4,2,8,128]{3,2,1,0:T(8,128)S(1)} %get-tuple-element.17), channel_id=1, source_target_pairs={{64,112},{68,116},{72,120},{76,124},{65,113},{69,117},{73,121},{77... | collective-permute-start | bytes 98312 | tf_op jit(solution)/shard_map/cond/branch_1_fun/ppermute | solution.py:263
  75.5 1.0 %collective-permute-done = f32[4,2,8,128]{3,2,1,0:T(8,128)S(1)} collective-permute-done((f32[4,2,8,128]{3,2,1,0:T(8,128)S(1)}, f32[4,2,8,128]{3,2,1,0:T(8,128)S(1)}, u32[]{:S(2)}, u32[]{:S(2)}) %collective-permute-start) | collective-permute-done | bytes 32800 | tf_op jit(solution)/shard_map/cond/branch_1_fun/ppermute | solution.py:263
  77.2 0.7 collective-permute-start.2
  78.7 1.3 %collective-permute-start.4 = (f32[2,8,128]{2,1,0:T(8,128)S(1)}, f32[2,8,128]{2,1,0:T(8,128)S(1)}, u32[]{:S(2)}, u32[]{:S(2)}) collective-permute-start(f32[2,8,128]{2,1,0:T(8,128)S(1)} %fusion.1), channel_id=1, source_target_pairs={{112,144},{116,148},{120,152},{124,156},{176,208},{180,212},{184,2... | collective-permute-start | bytes 24584 | tf_op jit(solution)/shard_map/cond/branch_1_fun/ppermute | solution.py:263
  80.0 1.3 %collective-permute-start.5 = (f32[2,8,128]{2,1,0:T(8,128)S(1)}, f32[2,8,128]{2,1,0:T(8,128)S(1)}, u32[]{:S(2)}, u32[]{:S(2)}) collective-permute-start(f32[2,8,128]{2,1,0:T(8,128)S(1)} %fusion.1), channel_id=1, source_target_pairs={{112,160},{116,164},{120,168},{124,172},{176,224},{180,228},{184,2... | collective-permute-start | bytes 24584 | tf_op jit(solution)/shard_map/cond/branch_1_fun/ppermute | solution.py:263
  81.3 0.7 collective-permute-done.5
  82.1 15.0 %all_to_all.10 = f32[16,2,2,8,128]{4,3,2,1,0:T(8,128)S(1)} all-to-all(f32[16,2,2,8,128]{4,3,2,1,0:T(8,128)S(1)} %bitcast.18), channel_id=1, replica_groups={{0,1,2,3,4,5,6,7,8,9,10,11,12,13,14,15},{16,17,18,19,20,21,22,23,24,25,..., dimensions={0} | all-to-all | bytes 524288 | tf_op jit(solution)/shard_map/all_to_all | solution.py:321
  97.1 2.6 %shard_map.50 = f32[4,8,8,128]{3,2,1,0:T(8,128)} custom-call(f32[4,4,2,2,8,128]{5,4,3,2,1,0:T(8,128)S(1)} %bitcast.19, f32[32,8,128]{2,1,0:T(8,128)S(1)} %get-tuple-element.35.prefix, f32[8,8,128]{2,1,0:T(8,128)S(1)} %get-tuple-element.36.added, f32[4,8,8,128]{3,2,1,0:T(8,128)S(1)} %get-tuple-element.37.held, f32[6,32,8,128]{3,2,1,0:T(8,128)S(1)} %get-tuple-element.31.coef, ...), custom_call_target="tpu_custom_call" | custom-call | tf_op jit(solution)/shard_map/pallas_call | solution.py:236
  (20 shorter events, 2.7 us)
Async XLA Ops:
  2.0 18.6 %all-to-all-start = ((f32[4,64,8,128]{3,2,1,0:T(8,128)}), f32[4,64,8,128]{3,2,1,0:T(8,128)S(1)}, u32[]{:S(2)}, u32[]{:S(2)}) async-start(f32[4,64,8,128]{3,2,1,0:T(8,128)} %broadcast_in_dim.16), calls=%async_computation | async-start | bytes 2097152 | tf_op jit(solution)/shard_map/all_to_all | solution.py:267
  22.2 8.0 %collective-permute-start.6 = (f32[32,8,128]{2,1,0:T(8,128)S(1)}, f32[32,8,128]{2,1,0:T(8,128)S(1)}, u32[]{:S(2)}, u32[]{:S(2)}) collective-permute-start(f32[32,8,128]{2,1,0:T(8,128)S(1)} %get-tuple-element.29), channel_id=1, source_target_pairs={{0,4},{4,8},{8,12},{12,16},{16,20},{20,24},{24,28},{28,32},{32,36}... | collective-permute-start | bytes 393224 | tf_op jit(solution)/shard_map/ppermute | solution.py:278
  43.6 9.1 %collective-permute-start.7 = (f32[7,2,8,128]{3,2,1,0:T(8,128)S(1)}, f32[7,2,8,128]{3,2,1,0:T(8,128)S(1)}, u32[]{:S(2)}, u32[]{:S(2)}) collective-permute-start(f32[7,2,8,128]{3,2,1,0:T(8,128)S(1)} %get-tuple-element.34), channel_id=1, source_target_pairs={{0,16},{4,20},{8,24},{12,28},{64,80},{68,84},{72,88},{76,92},{128,... | collective-permute-start | bytes 172040 | tf_op jit(solution)/shard_map/ppermute | solution.py:263
  51.4 2.6 %collective-permute-start.8 = (f32[7,2,8,128]{3,2,1,0:T(8,128)S(1)}, f32[7,2,8,128]{3,2,1,0:T(8,128)S(1)}, u32[]{:S(2)}, u32[]{:S(2)}) collective-permute-start(f32[7,2,8,128]{3,2,1,0:T(8,128)S(1)} %get-tuple-element.34), channel_id=1, source_target_pairs={{32,48},{36,52},{40,56},{44,60},{96,112},{100,116},{104,120},{108,... | collective-permute-start | bytes 172040 | tf_op jit(solution)/shard_map/ppermute | solution.py:263
  52.7 1.3 %collective-permute-start.10 = (f32[7,2,8,128]{3,2,1,0:T(8,128)S(1)}, f32[7,2,8,128]{3,2,1,0:T(8,128)S(1)}, u32[]{:S(2)}, u32[]{:S(2)}) collective-permute-start(f32[7,2,8,128]{3,2,1,0:T(8,128)S(1)} %add.45), channel_id=1, source_target_pairs={{16,32},{20,36},{24,40},{28,44},{80,96},{84,100},{88,104},{92,108}... | collective-permute-start | bytes 172040 | tf_op jit(solution)/shard_map/ppermute | solution.py:263
  53.3 0.7 collective-permute-start.9
  54.1 19.8 %collective-permute-start.11 = (f32[4,2,8,128]{3,2,1,0:T(8,128)S(1)}, f32[4,2,8,128]{3,2,1,0:T(8,128)S(1)}, u32[]{:S(2)}, u32[]{:S(2)}) collective-permute-start(f32[4,2,8,128]{3,2,1,0:T(8,128)S(1)} %slice.8), channel_id=1, source_target_pairs={{48,64},{52,68},{56,72},{60,76},{49,65},{53,69},{57,73},{61,77},{5... | collective-permute-start | bytes 98312 | tf_op jit(solution)/shard_map/ppermute | solution.py:263
  73.9 2.6 %collective-permute-start = (f32[4,2,8,128]{3,2,1,0:T(8,128)S(1)}, f32[4,2,8,128]{3,2,1,0:T(8,128)S(1)}, u32[]{:S(2)}, u32[]{:S(2)}) collective-permute-start(f32[4,2,8,128]{3,2,1,0:T(8,128)S(1)} %get-tuple-element.17), channel_id=1, source_target_pairs={{64,112},{68,116},{72,120},{76,124},{65,113},{69,117},{73,121},{77... | collective-permute-start | bytes 98312 | tf_op jit(solution)/shard_map/cond/branch_1_fun/ppermute | solution.py:263
  76.6 0.7 collective-permute-start.1
  77.2 0.7 collective-permute-start.2
  78.0 3.3 %collective-permute-start.3 = (f32[2,8,128]{2,1,0:T(8,128)S(1)}, f32[2,8,128]{2,1,0:T(8,128)S(1)}, u32[]{:S(2)}, u32[]{:S(2)}) collective-permute-start(f32[2,8,128]{2,1,0:T(8,128)S(1)} %fusion.1), channel_id=1, source_target_pairs={{112,128},{116,132},{120,136},{124,140},{176,192},{180,196},{184,2... | collective-permute-start | bytes 24584 | tf_op jit(solution)/shard_map/cond/branch_1_fun/ppermute | solution.py:263
  78.7 2.7 %collective-permute-start.4 = (f32[2,8,128]{2,1,0:T(8,128)S(1)}, f32[2,8,128]{2,1,0:T(8,128)S(1)}, u32[]{:S(2)}, u32[]{:S(2)}) collective-permute-start(f32[2,8,128]{2,1,0:T(8,128)S(1)} %fusion.1), channel_id=1, source_target_pairs={{112,144},{116,148},{120,152},{124,156},{176,208},{180,212},{184,2... | collective-permute-start | bytes 24584 | tf_op jit(solution)/shard_map/cond/branch_1_fun/ppermute | solution.py:263
  80.0 2.1 %collective-permute-start.5 = (f32[2,8,128]{2,1,0:T(8,128)S(1)}, f32[2,8,128]{2,1,0:T(8,128)S(1)}, u32[]{:S(2)}, u32[]{:S(2)}) collective-permute-start(f32[2,8,128]{2,1,0:T(8,128)S(1)} %fusion.1), channel_id=1, source_target_pairs={{112,160},{116,164},{120,168},{124,172},{176,224},{180,228},{184,2... | collective-permute-start | bytes 24584 | tf_op jit(solution)/shard_map/cond/branch_1_fun/ppermute | solution.py:263

commit v6 on v5

--- a/solution.py
+++ b/solution.py
@@ -164,16 +164,12 @@
         added[r] = jnp.where(end, fields[total, at], residuals[member, at])
 
 
-def share_kernel(parts, entry, send):
-    _, place2, _ = place()
-    inner = jnp.where(place2 > 0, 1.0, 0.0)
-    for j in range(parts.shape[1]):
-        outer = entry[j]
-        level2 = parts[jnp.maximum(place2 - 1, 0), j] * inner
+def share_kernel(level2, entry, send):
+    for j in range(entry.shape[0]):
         for a in range(send.shape[0]):
             for s in range(send.shape[1]):
-                send[a, s, 0, j] = outer
-                send[a, s, 1, j] = level2
+                send[a, s, 0, j] = entry[j]
+                send[a, s, 1, j] = level2[j]
 
 
 def final_kernel(received, prefix, added, held, coef, ab, out, v):
@@ -291,32 +287,71 @@
         mib=6,
     )
     ends = FACTOR - 1
-    third = hop(parts, [((w, 2), (w, 3)) for w in range(wides)])
-    pair = parts + hop(parts, [((w, 0), (w, 1)) for w in range(wides)])
-    to_last = hop(pair, [((w, 1), (w, 3)) for w in range(wides)])
-    to_next = hop(pair, [((w, 1), (w, 2)) for w in range(wides)])
-    parts = pair + third + to_last + to_next
-    goals = parts[FACTOR - 1 :]
-    first = hop(goals, [((0, ends), (1, 0))])
     rank = lax.axis_index("tm")
     wide = lax.div(rank, count // wides)
+    place2 = lax.rem(lax.div(rank, FACTOR), FACTOR)
+
+    def message(parts, start):
+        return lax.dynamic_slice(parts, (start, 0, 0, 0), (FACTOR + 1,) + parts.shape[1:])
+
+    def inside(value, pairs, block2s):
+        return hop(value, [((w, i), (w, j)) for w in block2s for i, j in pairs])
+
+    def direct(parts):
+        block2s = range(1)
+        summed = inside(parts[ends - 1 :], [(0, 3)], block2s)
+        summed = summed + inside(message(parts, jnp.minimum(place2 + 1, 2)), [(0, 2), (1, 3)], block2s)
+        summed = summed + inside(message(parts, jnp.minimum(place2, 2)), [(0, 1), (2, 3)], block2s)
+        summed = summed + inside(parts[1 : FACTOR + 2], [(1, 2)], block2s)
+        return (summed[0], *(parts[ends + i] + summed[1 + i] for i in range(FACTOR)))
+
+    def tree(parts):
+        block2s = range(1, wides)
+
+        def early(parts):
+            got = inside(parts, [(0, 1)], block2s)
+            return tuple(got[i] for i in range(2 * FACTOR - 1))
+
+        none = jnp.zeros_like(parts[0])
+        got = lax.cond(place2 <= 1, early, lambda parts: (none,) * (2 * FACTOR - 1), parts)
+        pair = parts + jnp.stack(got)
+
+        def late(pair, parts):
+            third = inside(parts[ends - 1 :], [(2, 3)], block2s)
+            fourth = inside(pair[ends - 1 :], [(1, 3)], block2s)
+            next_ = inside(pair[1], [(1, 2)], block2s)
+            both = third + fourth
+            return (both[0] + next_, *(both[1 + i] for i in range(FACTOR)))
+
+        first2, *got4 = lax.cond(place2 >= 1, late, lambda pair, parts: (none,) * (FACTOR + 1), pair, parts)
+        return (jnp.where(place2 == 1, got[0], first2), *(pair[ends + i] + got4[i] for i in range(FACTOR)))
+
+    level2, *goals = lax.cond(wide > 0, tree, direct, parts)
+    goals = jnp.stack(goals)
+    first = hop(goals, [((0, ends), (1, 0))])
 
     def carry_on(goals, first):
         entry = hop(first, [((1, 0), (1, ends))])
-        for w in range(1, wides - 1):
-            entry = entry + hop(goals + entry, [((w, ends), (w + 1, ends))])
-        leave = lax.dynamic_slice(goals + entry, (wide, 0, 0, 0), (1,) + goals.shape[1:])[0]
-        in_first = (wide == 1) & (lax.rem(lax.div(rank, FACTOR), FACTOR) == 0)
-        leave = jnp.where(in_first, first[0], leave)
-        handed = jnp.where(in_first, first[0], 0.0)
+
+        def between(goals, entry):
+            for w in range(1, wides - 1):
+                entry = entry + hop(goals + entry, [((w, ends), (w + 1, ends))])
+            size = (1,) + goals.shape[1:]
+            return (
+                lax.dynamic_slice(goals + entry, (wide, 0, 0, 0), size)[0],
+                lax.dynamic_slice(entry, (wide - 1, 0, 0, 0), size)[0],
+            )
+
+        leave, own = lax.cond(
+            place2 == ends, between, lambda goals, entry: (first[0], first[0]), goals, entry
+        )
         for i in range(ends):
             pairs = [((w, ends), (w + 1, i)) for w in range(1, wides - 1)]
-            handed = handed + hop(leave, pairs + ([((1, 0), (1, i))] if i else []))
-        last = lax.dynamic_slice(entry, (wide - 1, 0, 0, 0), (1,) + goals.shape[1:])[0]
-        return jnp.where(lax.rem(lax.div(rank, FACTOR), FACTOR) == ends, last, handed)
+            own = own + hop(leave, pairs + ([((1, 0), (1, i))] if i else []))
+        return own
 
     entry = lax.cond(wide > 0, carry_on, lambda goals, first: jnp.zeros_like(goals[0]), goals, first)
-    send = call(share_kernel, (parts, entry), field(FACTOR, slabs, 2, own_rows))
+    send = call(share_kernel, (level2, entry), field(FACTOR, slabs, 2, own_rows))
     send = send.reshape((FACTOR * slabs, 2, own_rows) + tile)
     received = lax.all_to_all(send, ("tm", "space"), 0, 0, axis_index_groups=square, tiled=True)
     received = received.reshape((FACTOR, slabs, 2, own_rows) + tile)

time: 100 us -> 95.4 us (0.954)
  the two profiles are of different devices: /device:TPU:545 before, /device:TPU:33 now
where the time goes in v6:
time: 95.4 us; the launch traced here: 94.7 us
  waiting for transfers between devices  42.6 us (45%)
  starting transfers between devices  21 us (22%)
  blocking collectives  19.1 us (20%)
  Pallas kernels  9.06 us (9%)
  local copies, waits for them, and re-layouts  1.08 us (1%)
  other arithmetic  1.01 us (1%)
    ppermute x1, waiting for transfers between devices, local(): before = lax.ppermute(last, 'tm', [(q, q + 1) for q in range(count - 1)])  32.5 us
    all_to_all x1, blocking collectives, local(): lax.all_to_all(send, ('tm', 'space'), 0, 0, axis_index_groups=square, til...  11.7 us
    ppermute x1, starting transfers between devices, local(): before = lax.ppermute(last, 'tm', [(q, q + 1) for q in range(count - 1)])  10.6 us
    all_to_all x1, waiting for transfers between devices, local(): lax.all_to_all(jnp.broadcast_to(own, (slabs,) + own.shape[1:]), 'space',...  9.09 us
    pallas_call x5, Pallas kernels, call(): pl.pallas_call(kernel, out_shape=outputs, in_specs=[SMEM if i in smem els...  9.06 us
    all_gather x1, blocking collectives, local(): residuals = lax.all_gather(residual, 'tm', axis_index_groups=near)  7.34 us
    ppermute x5, starting transfers between devices, hop(): return lax.ppermute(value, 'tm', moves)  5.25 us
    all_to_all x1, starting transfers between devices, local(): lax.all_to_all(jnp.broadcast_to(own, (slabs,) + own.shape[1:]), 'space',...  5.12 us
  transfers between devices with their start and end apart: 7, of which 3 were waited for; matrix products, arithmetic and copies ran while one was open for 0% of the time, Pallas kernels for 0%

profile of v6, /device:TPU:33, one launch (start us, length us, event | category | flops | bytes accessed | tf_op | source)
XLA Modules:
  0.0 94.7 jit_solution(17256587668391844903)
XLA Ops:
  0.0 1.0 %pad_maximum_fusion = f32[8,8,8,128]{3,2,1,0:T(8,128)S(1)} fusion(f32[1,8,8,128]{3,2,1,0:T(8,128)} %bitcast.66, f32[3,8,8,128]{3,2,1,0:T(8,128)} %param.16, f32[4,8,8,128]{3,2,1,0:T(8,128)} %param.14), kind=kLoop, calls=%fused_computation.40 | loop fusion | flops 131072 | bytes 524288 | tf_op jit(solution)/shard_map/concatenate | solution.py:261
  1.0 1.0 %broadcast_in_dim.12 = f32[4,64,8,128]{3,2,1,0:T(8,128)} broadcast(f32[64,8,128]{2,1,0:T(8,128)S(1)} %bitcast.64), dimensions={1,2,3} | broadcast | bytes 1310720 | tf_op jit(solution)/shard_map/broadcast_in_dim | solution.py:264
  2.0 5.1 %all-to-all-start = ((f32[4,64,8,128]{3,2,1,0:T(8,128)}), f32[4,64,8,128]{3,2,1,0:T(8,128)S(1)}, u32[]{:S(2)}, u32[]{:S(2)}) async-start(f32[4,64,8,128]{3,2,1,0:T(8,128)} %broadcast_in_dim.12), calls=%async_computation | async-start | bytes 2097152 | tf_op jit(solution)/shard_map/all_to_all | solution.py:263
  7.8 9.1 %all-to-all-done.gathered = f32[4,64,8,128]{3,2,1,0:T(8,128)S(1)} async-done(((f32[4,64,8,128]{3,2,1,0:T(8,128)}), f32[4,64,8,128]{3,2,1,0:T(8,128)S(1)}, u32[]{:S(2)}, u32[]{:S(2)}) %all-to-all-start) | async-done | bytes 1048608 | tf_op jit(solution)/shard_map/all_to_all | solution.py:263
  16.9 1.6 %shard_map.46 = (f32[32,8,128]{2,1,0:T(8,128)S(1)}, f32[4,8,8,128]{3,2,1,0:T(8,128)S(1)}, f32[6,32,8,128]{3,2,1,0:T(8,128)S(1)}, f32[4,2,8,128]{3,2,1,0:T(8,128)S(1)}) custom-call(f32[1]{0:T(128)S(6)} %copy.56.kappa, f32[4,64,8,128]{3,2,1,0:T(8,128)S(1)} %all-to-all-done.gathered), custom_call_target="tpu_custom_call" | custom-call | tf_op jit(solution)/shard_map/pallas_call | solution.py:232
  18.5 10.6 %collective-permute-start.14 = (f32[32,8,128]{2,1,0:T(8,128)S(1)}, f32[32,8,128]{2,1,0:T(8,128)S(1)}, u32[]{:S(2)}, u32[]{:S(2)}) collective-permute-start(f32[32,8,128]{2,1,0:T(8,128)S(1)} %get-tuple-element.97), channel_id=1, source_target_pairs={{0,4},{4,8},{8,12},{12,16},{16,20},{20,24},{24,28},{28,32},{32,36}... | collective-permute-start | bytes 393224 | tf_op jit(solution)/shard_map/ppermute | solution.py:274
  29.1 32.5 %collective-permute-done.14.before = f32[32,8,128]{2,1,0:T(8,128)S(1)} collective-permute-done((f32[32,8,128]{2,1,0:T(8,128)S(1)}, f32[32,8,128]{2,1,0:T(8,128)S(1)}, u32[]{:S(2)}, u32[]{:S(2)}) %collective-permute-start.14) | collective-permute-done | bytes 131104 | tf_op jit(solution)/shard_map/ppermute | solution.py:274
  61.6 1.5 %shard_map.47 = (f32[32,8,128]{2,1,0:T(8,128)S(1)}, f32[4,8,8,128]{3,2,1,0:T(8,128)S(1)}) custom-call(f32[32,8,128]{2,1,0:T(8,128)S(1)} %collective-permute-done.14.before, f32[4,8,8,128]{3,2,1,0:T(8,128)S(1)} %get-tuple-element.98.kept, f32[6,32,8,128]{3,2,1,0:T(8,128)S(1)} %get-tuple-element.99.coef, f32[4,2,8,128]{3,2,1,0:T(8,128)S(1)} %get-tuple-element.100.ab), custom_call_target="tpu_custom_call" | custom-call | tf_op jit(solution)/shard_map/pallas_call | solution.py:232
  63.1 7.3 %all-gather = f32[128,8,128]{2,1,0:T(8,128)S(1)} all-gather(f32[32,8,128]{2,1,0:T(8,128)S(1)} %get-tuple-element.101), channel_id=2, replica_groups={{0,4,8,12},{16,20,24,28},{32,36,40,44},{48,52,56,60},{64,68,72,76},{80,..., dimensions={0}, use_global_device_ids=true | all-gather | bytes 655360 | tf_op jit(solution)/shard_map/all_gather | solution.py:281
  70.4 3.4 %shard_map.48 = (f32[7,2,8,128]{3,2,1,0:T(8,128)S(1)}, f32[32,8,128]{2,1,0:T(8,128)S(1)}, f32[8,8,128]{2,1,0:T(8,128)S(1)}) custom-call(f32[4,32,8,128]{3,2,1,0:T(8,128)S(1)} %bitcast.61, f32[6,32,8,128]{3,2,1,0:T(8,128)S(1)} %get-tuple-element.99.coef, f32[4,2,8,128]{3,2,1,0:T(8,128)S(1)} %get-tuple-element.100.ab), custom_call_target="tpu_custom_call" | custom-call | tf_op jit(solution)/shard_map/pallas_call | solution.py:232
  73.8 5.8 %conditional.5 = (f32[2,8,128]{2,1,0:T(8,128)S(1)}, f32[1,2,8,128]{3,2,1,0:T(8,128)S(1)}, f32[1,2,8,128]{3,2,1,0:T(8,128)S(1)}, f32[1,2,8,128]{3,2,1,0:T(8,128)S(1)}, f32[1,2,8,128]{3,2,1,0:T(8,128)S(1)}) conditional(s32[]{:T(128)} %convert_element_type.13, (f32[7,2,8,128]{3,2,1,0:T(8,128)S(1)}, s32[]{:T(128)}) %tuple.79, (s32[]{:T(128)}, ...), branch_computations={%region_0.0_spmd, %region_1.6_spmd} | conditional | flops 38921 | bytes 1589662 | solution.py:329
  73.9 1.3 %collective-permute-start.1 = (f32[5,2,8,128]{3,2,1,0:T(8,128)S(1)}, f32[5,2,8,128]{3,2,1,0:T(8,128)S(1)}, u32[]{:S(2)}, u32[]{:S(2)}) collective-permute-start(f32[5,2,8,128]{3,2,1,0:T(8,128)S(1)} %get-tuple-element.128), channel_id=1, source_target_pairs={{0,32},{4,36},{8,40},{12,44},{16,48},{20,52},{24,56},{28,60},{1,33... | collective-permute-start | bytes 122888 | tf_op jit(solution)/shard_map/cond/branch_0_fun/ppermute | solution.py:259
  75.2 0.7 collective-permute-start.3
  75.9 1.3 %collective-permute-start.2 = (f32[5,2,8,128]{3,2,1,0:T(8,128)S(1)}, f32[5,2,8,128]{3,2,1,0:T(8,128)S(1)}, u32[]{:S(2)}, u32[]{:S(2)}) collective-permute-start(f32[5,2,8,128]{3,2,1,0:T(8,128)S(1)} %get-tuple-element.130), channel_id=1, source_target_pairs={{0,16},{4,20},{8,24},{12,28},{32,48},{36,52},{40,56},{44,60},{1,17... | collective-permute-start | bytes 122888 | tf_op jit(solution)/shard_map/cond/branch_0_fun/ppermute | solution.py:259
  77.2 1.3 %collective-permute-start = (f32[5,2,8,128]{3,2,1,0:T(8,128)S(1)}, f32[5,2,8,128]{3,2,1,0:T(8,128)S(1)}, u32[]{:S(2)}, u32[]{:S(2)}) collective-permute-start(f32[5,2,8,128]{3,2,1,0:T(8,128)S(1)} %get-tuple-element.131), channel_id=1, source_target_pairs={{0,48},{4,52},{8,56},{12,60},{1,49},{5,53},{9,57},{13,61},{2,50},{... | collective-permute-start | bytes 122888 | tf_op jit(solution)/shard_map/cond/branch_0_fun/ppermute | solution.py:259
  78.5 0.0 collective-permute-done.1
  78.5 0.0 collective-permute-done.3
  78.5 0.0 collective-permute-done.2
  78.5 1.0 %collective-permute-done = f32[5,2,8,128]{3,2,1,0:T(8,128)S(1)} collective-permute-done((f32[5,2,8,128]{3,2,1,0:T(8,128)S(1)}, f32[5,2,8,128]{3,2,1,0:T(8,128)S(1)}, u32[]{:S(2)}, u32[]{:S(2)}) %collective-permute-start) | collective-permute-done | bytes 40992 | tf_op jit(solution)/shard_map/cond/branch_0_fun/ppermute | solution.py:259
  79.7 0.7 collective-permute-start.15
  80.3 0.0 collective-permute-done.15
  80.4 11.7 %all_to_all.10 = f32[16,2,2,8,128]{4,3,2,1,0:T(8,128)S(1)} all-to-all(f32[16,2,2,8,128]{4,3,2,1,0:T(8,128)S(1)} %bitcast.62), channel_id=1, replica_groups={{0,1,2,3,4,5,6,7,8,9,10,11,12,13,14,15},{16,17,18,19,20,21,22,23,24,25,..., dimensions={0} | all-to-all | bytes 524288 | tf_op jit(solution)/shard_map/all_to_all | solution.py:356
  92.1 2.6 %shard_map.50 = f32[4,8,8,128]{3,2,1,0:T(8,128)} custom-call(f32[4,4,2,2,8,128]{5,4,3,2,1,0:T(8,128)S(1)} %bitcast.63, f32[32,8,128]{2,1,0:T(8,128)S(1)} %get-tuple-element.108.prefix, f32[8,8,128]{2,1,0:T(8,128)S(1)} %get-tuple-element.109.added, f32[4,8,8,128]{3,2,1,0:T(8,128)S(1)} %get-tuple-element.110.held, ...), custom_call_target="tpu_custom_call" | custom-call | tf_op jit(solution)/shard_map/pallas_call | solution.py:232
  (10 shorter events, 0.1 us)
Async XLA Ops:
  2.0 14.9 %all-to-all-start = ((f32[4,64,8,128]{3,2,1,0:T(8,128)}), f32[4,64,8,128]{3,2,1,0:T(8,128)S(1)}, u32[]{:S(2)}, u32[]{:S(2)}) async-start(f32[4,64,8,128]{3,2,1,0:T(8,128)} %broadcast_in_dim.12), calls=%async_computation | async-start | bytes 2097152 | tf_op jit(solution)/shard_map/all_to_all | solution.py:263
  18.5 43.1 %collective-permute-start.14 = (f32[32,8,128]{2,1,0:T(8,128)S(1)}, f32[32,8,128]{2,1,0:T(8,128)S(1)}, u32[]{:S(2)}, u32[]{:S(2)}) collective-permute-start(f32[32,8,128]{2,1,0:T(8,128)S(1)} %get-tuple-element.97), channel_id=1, source_target_pairs={{0,4},{4,8},{8,12},{12,16},{16,20},{20,24},{24,28},{28,32},{32,36}... | collective-permute-start | bytes 393224 | tf_op jit(solution)/shard_map/ppermute | solution.py:274
  73.9 4.6 %collective-permute-start.1 = (f32[5,2,8,128]{3,2,1,0:T(8,128)S(1)}, f32[5,2,8,128]{3,2,1,0:T(8,128)S(1)}, u32[]{:S(2)}, u32[]{:S(2)}) collective-permute-start(f32[5,2,8,128]{3,2,1,0:T(8,128)S(1)} %get-tuple-element.128), channel_id=1, source_target_pairs={{0,32},{4,36},{8,40},{12,44},{16,48},{20,52},{24,56},{28,60},{1,33... | collective-permute-start | bytes 122888 | tf_op jit(solution)/shard_map/cond/branch_0_fun/ppermute | solution.py:259
  75.2 3.3 %collective-permute-start.3 = (f32[5,2,8,128]{3,2,1,0:T(8,128)S(1)}, f32[5,2,8,128]{3,2,1,0:T(8,128)S(1)}, u32[]{:S(2)}, u32[]{:S(2)}) collective-permute-start(f32[5,2,8,128]{3,2,1,0:T(8,128)S(1)} %get-tuple-element.129), channel_id=1, source_target_pairs={{16,32},{20,36},{24,40},{28,44},{17,33},{21,37},{25,41},{29,45},{1... | collective-permute-start | bytes 122888 | tf_op jit(solution)/shard_map/cond/branch_0_fun/ppermute | solution.py:259
  75.9 2.7 %collective-permute-start.2 = (f32[5,2,8,128]{3,2,1,0:T(8,128)S(1)}, f32[5,2,8,128]{3,2,1,0:T(8,128)S(1)}, u32[]{:S(2)}, u32[]{:S(2)}) collective-permute-start(f32[5,2,8,128]{3,2,1,0:T(8,128)S(1)} %get-tuple-element.130), channel_id=1, source_target_pairs={{0,16},{4,20},{8,24},{12,28},{32,48},{36,52},{40,56},{44,60},{1,17... | collective-permute-start | bytes 122888 | tf_op jit(solution)/shard_map/cond/branch_0_fun/ppermute | solution.py:259
  77.2 2.4 %collective-permute-start = (f32[5,2,8,128]{3,2,1,0:T(8,128)S(1)}, f32[5,2,8,128]{3,2,1,0:T(8,128)S(1)}, u32[]{:S(2)}, u32[]{:S(2)}) collective-permute-start(f32[5,2,8,128]{3,2,1,0:T(8,128)S(1)} %get-tuple-element.131), channel_id=1, source_target_pairs={{0,48},{4,52},{8,56},{12,60},{1,49},{5,53},{9,57},{13,61},{2,50},{... | collective-permute-start | bytes 122888 | tf_op jit(solution)/shard_map/cond/branch_0_fun/ppermute | solution.py:259
  79.7 0.7 collective-permute-start.15

commit v7 on v6

--- a/solution.py
+++ b/solution.py
@@ -144,7 +144,7 @@
         step(src, n + 1, jnp.where(n < 7, 2, 3), lambda r, value: value)
         return carry
 
-    lax.fori_loop(4, 10, powers, 0)
+    lax.fori_loop(4, 9, powers, 0)
 
     def store(slot, source):
         for j in range(own):
@@ -153,7 +153,7 @@
     for later in range(1, FACTOR):
         n = later - 1 - place2
         store(later - 1, jnp.where(n >= 0, total + n, 0))
-    for goal in range(FACTOR):
+    for goal in range(FACTOR - 1):
         n = goal - wide
         store(FACTOR - 1 + goal, jnp.where(n < 0, 0, jnp.where(n == 0, z, 7 + n)))
     for r in range(rows):
@@ -282,8 +282,8 @@
     parts, prefix, added = call(
         spread_kernel,
         (residuals, coef, ab),
-        (field(2 * FACTOR - 1, own_rows), field(rows), field(rows_slab)),
-        scratch=[(11, rows) + tile],
+        (field(2 * FACTOR - 2, own_rows), field(rows), field(rows_slab)),
+        scratch=[(10, rows) + tile],
         mib=6,
     )
     ends = FACTOR - 1
@@ -292,7 +292,7 @@
     place2 = lax.rem(lax.div(rank, FACTOR), FACTOR)
 
     def message(parts, start):
-        return lax.dynamic_slice(parts, (start, 0, 0, 0), (FACTOR + 1,) + parts.shape[1:])
+        return lax.dynamic_slice(parts, (start, 0, 0, 0), (FACTOR,) + parts.shape[1:])
 
     def inside(value, pairs, block2s):
         return hop(value, [((w, i), (w, j)) for w in block2s for i, j in pairs])
@@ -302,18 +302,18 @@
         summed = inside(parts[ends - 1 :], [(0, 3)], block2s)
         summed = summed + inside(message(parts, jnp.minimum(place2 + 1, 2)), [(0, 2), (1, 3)], block2s)
         summed = summed + inside(message(parts, jnp.minimum(place2, 2)), [(0, 1), (2, 3)], block2s)
-        summed = summed + inside(parts[1 : FACTOR + 2], [(1, 2)], block2s)
-        return (summed[0], *(parts[ends + i] + summed[1 + i] for i in range(FACTOR)))
+        summed = summed + inside(parts[1 : FACTOR + 1], [(1, 2)], block2s)
+        return (summed[0], *(parts[ends + i] + summed[1 + i] for i in range(FACTOR - 1)))
 
     def tree(parts):
         block2s = range(1, wides)
 
         def early(parts):
             got = inside(parts, [(0, 1)], block2s)
-            return tuple(got[i] for i in range(2 * FACTOR - 1))
+            return tuple(got[i] for i in range(2 * FACTOR - 2))
 
         none = jnp.zeros_like(parts[0])
-        got = lax.cond(place2 <= 1, early, lambda parts: (none,) * (2 * FACTOR - 1), parts)
+        got = lax.cond(place2 <= 1, early, lambda parts: (none,) * (2 * FACTOR - 2), parts)
         pair = parts + jnp.stack(got)
 
         def late(pair, parts):
@@ -321,10 +321,10 @@
             fourth = inside(pair[ends - 1 :], [(1, 3)], block2s)
             next_ = inside(pair[1], [(1, 2)], block2s)
             both = third + fourth
-            return (both[0] + next_, *(both[1 + i] for i in range(FACTOR)))
-
-        first2, *got4 = lax.cond(place2 >= 1, late, lambda pair, parts: (none,) * (FACTOR + 1), pair, parts)
-        return (jnp.where(place2 == 1, got[0], first2), *(pair[ends + i] + got4[i] for i in range(FACTOR)))
+            return (both[0] + next_, *(both[1 + i] for i in range(FACTOR - 1)))
+
+        first2, *got4 = lax.cond(place2 >= 1, late, lambda pair, parts: (none,) * FACTOR, pair, parts)
+        return (jnp.where(place2 == 1, got[0], first2), *(pair[ends + i] + got4[i] for i in range(FACTOR - 1)))
 
     level2, *goals = lax.cond(wide > 0, tree, direct, parts)
     goals = jnp.stack(goals)
@@ -335,7 +335,8 @@
 
         def between(goals, entry):
             for w in range(1, wides - 1):
-                entry = entry + hop(goals + entry, [((w, ends), (w + 1, ends))])
+                moved = hop(goals[w:] + entry[w:], [((w, ends), (w + 1, ends))])
+                entry = jnp.concatenate([entry[:w], entry[w:] + moved])
             size = (1,) + goals.shape[1:]
             return (
                 lax.dynamic_slice(goals + entry, (wide, 0, 0, 0), size)[0],

time: 95.4 us -> 94.3 us (0.988)
  no operation moved by 1% of the time
where the time goes in v7:
time: 94.3 us; the launch traced here: 93.4 us
  waiting for transfers between devices  42.5 us (45%)
  starting transfers between devices  21 us (22%)
  blocking collectives  18.3 us (19%)
  Pallas kernels  8.69 us (9%)
  local copies, waits for them, and re-layouts  1.06 us (1%)
  other arithmetic  1.01 us (1%)
    ppermute x1, waiting for transfers between devices, local(): before = lax.ppermute(last, 'tm', [(q, q + 1) for q in range(count - 1)])  32.5 us
    all_to_all x1, blocking collectives, local(): lax.all_to_all(send, ('tm', 'space'), 0, 0, axis_index_groups=square, til...  10.9 us
    ppermute x1, starting transfers between devices, local(): before = lax.ppermute(last, 'tm', [(q, q + 1) for q in range(count - 1)])  10.6 us
    all_to_all x1, waiting for transfers between devices, local(): lax.all_to_all(jnp.broadcast_to(own, (slabs,) + own.shape[1:]), 'space',...  9.09 us
    pallas_call x5, Pallas kernels, call(): pl.pallas_call(kernel, out_shape=outputs, in_specs=[SMEM if i in smem els...  8.69 us
    all_gather x1, blocking collectives, local(): residuals = lax.all_gather(residual, 'tm', axis_index_groups=near)  7.34 us
    ppermute x5, starting transfers between devices, hop(): return lax.ppermute(value, 'tm', moves)  5.24 us
    all_to_all x1, starting transfers between devices, local(): lax.all_to_all(jnp.broadcast_to(own, (slabs,) + own.shape[1:]), 'space',...  5.12 us
  transfers between devices with their start and end apart: 7, of which 3 were waited for; matrix products, arithmetic and copies ran while one was open for 0% of the time, Pallas kernels for 0%

profile of v7, /device:TPU:33, one launch (start us, length us, event | category | flops | bytes accessed | tf_op | source)
XLA Modules:
  0.0 93.4 jit_solution(15863724472583955268)
XLA Ops:
  0.0 1.0 %pad_maximum_fusion = f32[8,8,8,128]{3,2,1,0:T(8,128)S(1)} fusion(f32[1,8,8,128]{3,2,1,0:T(8,128)} %bitcast.56, f32[3,8,8,128]{3,2,1,0:T(8,128)} %param.16, f32[4,8,8,128]{3,2,1,0:T(8,128)} %param.14), kind=kLoop, calls=%fused_computation.41 | loop fusion | flops 131072 | bytes 524288 | tf_op jit(solution)/shard_map/concatenate | solution.py:261
  1.0 1.0 %broadcast_in_dim.12 = f32[4,64,8,128]{3,2,1,0:T(8,128)} broadcast(f32[64,8,128]{2,1,0:T(8,128)S(1)} %bitcast.54), dimensions={1,2,3} | broadcast | bytes 1310720 | tf_op jit(solution)/shard_map/broadcast_in_dim | solution.py:264
  2.0 5.1 %all-to-all-start = ((f32[4,64,8,128]{3,2,1,0:T(8,128)}), f32[4,64,8,128]{3,2,1,0:T(8,128)S(1)}, u32[]{:S(2)}, u32[]{:S(2)}) async-start(f32[4,64,8,128]{3,2,1,0:T(8,128)} %broadcast_in_dim.12), calls=%async_computation | async-start | bytes 2097152 | tf_op jit(solution)/shard_map/all_to_all | solution.py:263
  7.8 9.1 %all-to-all-done.gathered = f32[4,64,8,128]{3,2,1,0:T(8,128)S(1)} async-done(((f32[4,64,8,128]{3,2,1,0:T(8,128)}), f32[4,64,8,128]{3,2,1,0:T(8,128)S(1)}, u32[]{:S(2)}, u32[]{:S(2)}) %all-to-all-start) | async-done | bytes 1048608 | tf_op jit(solution)/shard_map/all_to_all | solution.py:263
  16.9 1.6 %shard_map.46 = (f32[32,8,128]{2,1,0:T(8,128)S(1)}, f32[4,8,8,128]{3,2,1,0:T(8,128)S(1)}, f32[6,32,8,128]{3,2,1,0:T(8,128)S(1)}, f32[4,2,8,128]{3,2,1,0:T(8,128)S(1)}) custom-call(f32[1]{0:T(128)S(6)} %copy.48.kappa, f32[4,64,8,128]{3,2,1,0:T(8,128)S(1)} %all-to-all-done.gathered), custom_call_target="tpu_custom_call" | custom-call | tf_op jit(solution)/shard_map/pallas_call | solution.py:232
  18.5 10.6 %collective-permute-start.14 = (f32[32,8,128]{2,1,0:T(8,128)S(1)}, f32[32,8,128]{2,1,0:T(8,128)S(1)}, u32[]{:S(2)}, u32[]{:S(2)}) collective-permute-start(f32[32,8,128]{2,1,0:T(8,128)S(1)} %get-tuple-element.98), channel_id=1, source_target_pairs={{0,4},{4,8},{8,12},{12,16},{16,20},{20,24},{24,28},{28,32},{32,36}... | collective-permute-start | bytes 393224 | tf_op jit(solution)/shard_map/ppermute | solution.py:274
  29.1 32.5 %collective-permute-done.14.before = f32[32,8,128]{2,1,0:T(8,128)S(1)} collective-permute-done((f32[32,8,128]{2,1,0:T(8,128)S(1)}, f32[32,8,128]{2,1,0:T(8,128)S(1)}, u32[]{:S(2)}, u32[]{:S(2)}) %collective-permute-start.14) | collective-permute-done | bytes 131104 | tf_op jit(solution)/shard_map/ppermute | solution.py:274
  61.6 1.5 %shard_map.47 = (f32[32,8,128]{2,1,0:T(8,128)S(1)}, f32[4,8,8,128]{3,2,1,0:T(8,128)S(1)}) custom-call(f32[32,8,128]{2,1,0:T(8,128)S(1)} %collective-permute-done.14.before, f32[4,8,8,128]{3,2,1,0:T(8,128)S(1)} %get-tuple-element.99.kept, f32[6,32,8,128]{3,2,1,0:T(8,128)S(1)} %get-tuple-element.100.coef, f32[4,2,8,128]{3,2,1,0:T(8,128)S(1)} %get-tuple-element.101.ab), custom_call_target="tpu_custom_call" | custom-call | tf_op jit(solution)/shard_map/pallas_call | solution.py:232
  63.1 7.3 %all-gather = f32[128,8,128]{2,1,0:T(8,128)S(1)} all-gather(f32[32,8,128]{2,1,0:T(8,128)S(1)} %get-tuple-element.102), channel_id=2, replica_groups={{0,4,8,12},{16,20,24,28},{32,36,40,44},{48,52,56,60},{64,68,72,76},{80,..., dimensions={0}, use_global_device_ids=true | all-gather | bytes 655360 | tf_op jit(solution)/shard_map/all_gather | solution.py:281
  70.4 3.0 %shard_map.48 = (f32[6,2,8,128]{3,2,1,0:T(8,128)S(1)}, f32[32,8,128]{2,1,0:T(8,128)S(1)}, f32[8,8,128]{2,1,0:T(8,128)S(1)}) custom-call(f32[4,32,8,128]{3,2,1,0:T(8,128)S(1)} %bitcast.51, f32[6,32,8,128]{3,2,1,0:T(8,128)S(1)} %get-tuple-element.100.coef, f32[4,2,8,128]{3,2,1,0:T(8,128)S(1)} %get-tuple-element.101.ab), custom_call_target="tpu_custom_call" | custom-call | tf_op jit(solution)/shard_map/pallas_call | solution.py:232
  73.4 5.7 %conditional.5 = (f32[2,8,128]{2,1,0:T(8,128)S(1)}, f32[1,2,8,128]{3,2,1,0:T(8,128)S(1)}, f32[1,2,8,128]{3,2,1,0:T(8,128)S(1)}, f32[1,2,8,128]{3,2,1,0:T(8,128)S(1)}) conditional(s32[]{:T(128)} %convert_element_type.13, (f32[6,2,8,128]{3,2,1,0:T(8,128)S(1)}, s32[]{:T(128)}) %tuple.75, (s32[]{:T(128)}, f32[6,2,8,128]{3,2,1,0:T(8,128)S(1)}) %tuple.76), branch_computations={%region_0.0_spmd, %region_1.6_spmd} | conditional | flops 30729 | bytes 1335686 | solution.py:329
  73.5 1.3 %collective-permute-start.1 = (f32[4,2,8,128]{3,2,1,0:T(8,128)S(1)}, f32[4,2,8,128]{3,2,1,0:T(8,128)S(1)}, u32[]{:S(2)}, u32[]{:S(2)}) collective-permute-start(f32[4,2,8,128]{3,2,1,0:T(8,128)S(1)} %get-tuple-element.124), channel_id=1, source_target_pairs={{0,32},{4,36},{8,40},{12,44},{16,48},{20,52},{24,56},{28,60},{1,33... | collective-permute-start | bytes 98312 | tf_op jit(solution)/shard_map/cond/branch_0_fun/ppermute | solution.py:259
  74.8 0.7 collective-permute-start.3
  75.5 1.3 %collective-permute-start.2 = (f32[4,2,8,128]{3,2,1,0:T(8,128)S(1)}, f32[4,2,8,128]{3,2,1,0:T(8,128)S(1)}, u32[]{:S(2)}, u32[]{:S(2)}) collective-permute-start(f32[4,2,8,128]{3,2,1,0:T(8,128)S(1)} %get-tuple-element.126), channel_id=1, source_target_pairs={{0,16},{4,20},{8,24},{12,28},{32,48},{36,52},{40,56},{44,60},{1,17... | collective-permute-start | bytes 98312 | tf_op jit(solution)/shard_map/cond/branch_0_fun/ppermute | solution.py:259
  76.8 1.3 %collective-permute-start = (f32[4,2,8,128]{3,2,1,0:T(8,128)S(1)}, f32[4,2,8,128]{3,2,1,0:T(8,128)S(1)}, u32[]{:S(2)}, u32[]{:S(2)}) collective-permute-start(f32[4,2,8,128]{3,2,1,0:T(8,128)S(1)} %get-tuple-element.127), channel_id=1, source_target_pairs={{0,48},{4,52},{8,56},{12,60},{1,49},{5,53},{9,57},{13,61},{2,50},{... | collective-permute-start | bytes 98312 | tf_op jit(solution)/shard_map/cond/branch_0_fun/ppermute | solution.py:259
  78.1 0.0 collective-permute-done.1
  78.1 0.0 collective-permute-done.3
  78.1 0.0 collective-permute-done.2
  78.1 1.0 %collective-permute-done = f32[4,2,8,128]{3,2,1,0:T(8,128)S(1)} collective-permute-done((f32[4,2,8,128]{3,2,1,0:T(8,128)S(1)}, f32[4,2,8,128]{3,2,1,0:T(8,128)S(1)}, u32[]{:S(2)}, u32[]{:S(2)}) %collective-permute-start) | collective-permute-done | bytes 32800 | tf_op jit(solution)/shard_map/cond/branch_0_fun/ppermute | solution.py:259
  79.2 0.7 collective-permute-start.15
  79.8 0.0 collective-permute-done.15
  79.9 10.9 %all_to_all.10 = f32[16,2,2,8,128]{4,3,2,1,0:T(8,128)S(1)} all-to-all(f32[16,2,2,8,128]{4,3,2,1,0:T(8,128)S(1)} %bitcast.52), channel_id=1, replica_groups={{0,1,2,3,4,5,6,7,8,9,10,11,12,13,14,15},{16,17,18,19,20,21,22,23,24,25,..., dimensions={0} | all-to-all | bytes 524288 | tf_op jit(solution)/shard_map/all_to_all | solution.py:357
  90.8 2.6 %shard_map.50 = f32[4,8,8,128]{3,2,1,0:T(8,128)} custom-call(f32[4,4,2,2,8,128]{5,4,3,2,1,0:T(8,128)S(1)} %bitcast.53, f32[32,8,128]{2,1,0:T(8,128)S(1)} %get-tuple-element.108.prefix, f32[8,8,128]{2,1,0:T(8,128)S(1)} %get-tuple-element.109.added, f32[4,8,8,128]{3,2,1,0:T(8,128)S(1)} %get-tuple-element.110.held, ...), custom_call_target="tpu_custom_call" | custom-call | tf_op jit(solution)/shard_map/pallas_call | solution.py:232
  (9 shorter events, 0.1 us)
Async XLA Ops:
  2.0 14.9 %all-to-all-start = ((f32[4,64,8,128]{3,2,1,0:T(8,128)}), f32[4,64,8,128]{3,2,1,0:T(8,128)S(1)}, u32[]{:S(2)}, u32[]{:S(2)}) async-start(f32[4,64,8,128]{3,2,1,0:T(8,128)} %broadcast_in_dim.12), calls=%async_computation | async-start | bytes 2097152 | tf_op jit(solution)/shard_map/all_to_all | solution.py:263
  18.5 43.1 %collective-permute-start.14 = (f32[32,8,128]{2,1,0:T(8,128)S(1)}, f32[32,8,128]{2,1,0:T(8,128)S(1)}, u32[]{:S(2)}, u32[]{:S(2)}) collective-permute-start(f32[32,8,128]{2,1,0:T(8,128)S(1)} %get-tuple-element.98), channel_id=1, source_target_pairs={{0,4},{4,8},{8,12},{12,16},{16,20},{20,24},{24,28},{28,32},{32,36}... | collective-permute-start | bytes 393224 | tf_op jit(solution)/shard_map/ppermute | solution.py:274
  73.5 4.6 %collective-permute-start.1 = (f32[4,2,8,128]{3,2,1,0:T(8,128)S(1)}, f32[4,2,8,128]{3,2,1,0:T(8,128)S(1)}, u32[]{:S(2)}, u32[]{:S(2)}) collective-permute-start(f32[4,2,8,128]{3,2,1,0:T(8,128)S(1)} %get-tuple-element.124), channel_id=1, source_target_pairs={{0,32},{4,36},{8,40},{12,44},{16,48},{20,52},{24,56},{28,60},{1,33... | collective-permute-start | bytes 98312 | tf_op jit(solution)/shard_map/cond/branch_0_fun/ppermute | solution.py:259
  74.8 3.3 %collective-permute-start.3 = (f32[4,2,8,128]{3,2,1,0:T(8,128)S(1)}, f32[4,2,8,128]{3,2,1,0:T(8,128)S(1)}, u32[]{:S(2)}, u32[]{:S(2)}) collective-permute-start(f32[4,2,8,128]{3,2,1,0:T(8,128)S(1)} %get-tuple-element.125), channel_id=1, source_target_pairs={{16,32},{20,36},{24,40},{28,44},{17,33},{21,37},{25,41},{29,45},{1... | collective-permute-start | bytes 98312 | tf_op jit(solution)/shard_map/cond/branch_0_fun/ppermute | solution.py:259
  75.5 2.7 %collective-permute-start.2 = (f32[4,2,8,128]{3,2,1,0:T(8,128)S(1)}, f32[4,2,8,128]{3,2,1,0:T(8,128)S(1)}, u32[]{:S(2)}, u32[]{:S(2)}) collective-permute-start(f32[4,2,8,128]{3,2,1,0:T(8,128)S(1)} %get-tuple-element.126), channel_id=1, source_target_pairs={{0,16},{4,20},{8,24},{12,28},{32,48},{36,52},{40,56},{44,60},{1,17... | collective-permute-start | bytes 98312 | tf_op jit(solution)/shard_map/cond/branch_0_fun/ppermute | solution.py:259
  76.8 2.3 %collective-permute-start = (f32[4,2,8,128]{3,2,1,0:T(8,128)S(1)}, f32[4,2,8,128]{3,2,1,0:T(8,128)S(1)}, u32[]{:S(2)}, u32[]{:S(2)}) collective-permute-start(f32[4,2,8,128]{3,2,1,0:T(8,128)S(1)} %get-tuple-element.127), channel_id=1, source_target_pairs={{0,48},{4,52},{8,56},{12,60},{1,49},{5,53},{9,57},{13,61},{2,50},{... | collective-permute-start | bytes 98312 | tf_op jit(solution)/shard_map/cond/branch_0_fun/ppermute | solution.py:259
  79.2 0.7 collective-permute-start.15

commit v8 on v7

--- a/solution.py
+++ b/solution.py
@@ -139,12 +139,17 @@
     total = FACTOR
     z = total + FACTOR - 1 - place2
 
-    def powers(n, carry):
-        src = jnp.where(n == 7, z, n)
-        step(src, n + 1, jnp.where(n < 7, 2, 3), lambda r, value: value)
-        return carry
-
-    lax.fori_loop(4, 9, powers, 0)
+    def twos(n, carry):
+        step(n, n + 1, 2, lambda r, value: value)
+        return carry
+
+    lax.fori_loop(total, z, twos, 0)
+
+    def threes(n, carry):
+        step(jnp.where(n == 7, z, n), n + 1, 3, lambda r, value: value)
+        return carry
+
+    lax.fori_loop(7, 7 + jnp.maximum(FACTOR - 2 - wide, 0), threes, 0)
 
     def store(slot, source):
         for j in range(own):

time: 94.3 us -> 93.9 us (level)
  no operation moved by 1% of the time
where the time goes in v8:
time: 93.9 us; the launch traced here: 93.4 us
  waiting for transfers between devices  42.5 us (45%)
  starting transfers between devices  21 us (22%)
  blocking collectives  18.3 us (19%)
  Pallas kernels  8.68 us (9%)
  local copies, waits for them, and re-layouts  1.06 us (1%)
  other arithmetic  1.01 us (1%)
    ppermute x1, waiting for transfers between devices, local(): before = lax.ppermute(last, 'tm', [(q, q + 1) for q in range(count - 1)])  32.5 us
    all_to_all x1, blocking collectives, local(): lax.all_to_all(send, ('tm', 'space'), 0, 0, axis_index_groups=square, til...  10.9 us
    ppermute x1, starting transfers between devices, local(): before = lax.ppermute(last, 'tm', [(q, q + 1) for q in range(count - 1)])  10.6 us
    all_to_all x1, waiting for transfers between devices, local(): lax.all_to_all(jnp.broadcast_to(own, (slabs,) + own.shape[1:]), 'space',...  9.09 us
    pallas_call x5, Pallas kernels, call(): pl.pallas_call(kernel, out_shape=outputs, in_specs=[SMEM if i in smem els...  8.68 us
    all_gather x1, blocking collectives, local(): residuals = lax.all_gather(residual, 'tm', axis_index_groups=near)  7.34 us
    ppermute x5, starting transfers between devices, hop(): return lax.ppermute(value, 'tm', moves)  5.24 us
    all_to_all x1, starting transfers between devices, local(): lax.all_to_all(jnp.broadcast_to(own, (slabs,) + own.shape[1:]), 'space',...  5.12 us
  transfers between devices with their start and end apart: 7, of which 3 were waited for; matrix products, arithmetic and copies ran while one was open for 0% of the time, Pallas kernels for 0%

profile of v8, /device:TPU:33, one launch (start us, length us, event | category | flops | bytes accessed | tf_op | source)
XLA Modules:
  0.0 93.4 jit_solution(17542480928489290188)
XLA Ops:
  0.0 1.0 %pad_maximum_fusion = f32[8,8,8,128]{3,2,1,0:T(8,128)S(1)} fusion(f32[1,8,8,128]{3,2,1,0:T(8,128)} %bitcast.56, f32[3,8,8,128]{3,2,1,0:T(8,128)} %param.16, f32[4,8,8,128]{3,2,1,0:T(8,128)} %param.14), kind=kLoop, calls=%fused_computation.41 | loop fusion | flops 131072 | bytes 524288 | tf_op jit(solution)/shard_map/concatenate | solution.py:266
  1.0 1.0 %broadcast_in_dim.12 = f32[4,64,8,128]{3,2,1,0:T(8,128)} broadcast(f32[64,8,128]{2,1,0:T(8,128)S(1)} %bitcast.54), dimensions={1,2,3} | broadcast | bytes 1310720 | tf_op jit(solution)/shard_map/broadcast_in_dim | solution.py:269
  2.0 5.1 %all-to-all-start = ((f32[4,64,8,128]{3,2,1,0:T(8,128)}), f32[4,64,8,128]{3,2,1,0:T(8,128)S(1)}, u32[]{:S(2)}, u32[]{:S(2)}) async-start(f32[4,64,8,128]{3,2,1,0:T(8,128)} %broadcast_in_dim.12), calls=%async_computation | async-start | bytes 2097152 | tf_op jit(solution)/shard_map/all_to_all | solution.py:268
  7.8 9.1 %all-to-all-done.gathered = f32[4,64,8,128]{3,2,1,0:T(8,128)S(1)} async-done(((f32[4,64,8,128]{3,2,1,0:T(8,128)}), f32[4,64,8,128]{3,2,1,0:T(8,128)S(1)}, u32[]{:S(2)}, u32[]{:S(2)}) %all-to-all-start) | async-done | bytes 1048608 | tf_op jit(solution)/shard_map/all_to_all | solution.py:268
  16.9 1.6 %shard_map.46 = (f32[32,8,128]{2,1,0:T(8,128)S(1)}, f32[4,8,8,128]{3,2,1,0:T(8,128)S(1)}, f32[6,32,8,128]{3,2,1,0:T(8,128)S(1)}, f32[4,2,8,128]{3,2,1,0:T(8,128)S(1)}) custom-call(f32[1]{0:T(128)S(6)} %copy.48.kappa, f32[4,64,8,128]{3,2,1,0:T(8,128)S(1)} %all-to-all-done.gathered), custom_call_target="tpu_custom_call" | custom-call | tf_op jit(solution)/shard_map/pallas_call | solution.py:237
  18.5 10.6 %collective-permute-start.14 = (f32[32,8,128]{2,1,0:T(8,128)S(1)}, f32[32,8,128]{2,1,0:T(8,128)S(1)}, u32[]{:S(2)}, u32[]{:S(2)}) collective-permute-start(f32[32,8,128]{2,1,0:T(8,128)S(1)} %get-tuple-element.98), channel_id=1, source_target_pairs={{0,4},{4,8},{8,12},{12,16},{16,20},{20,24},{24,28},{28,32},{32,36}... | collective-permute-start | bytes 393224 | tf_op jit(solution)/shard_map/ppermute | solution.py:279
  29.1 32.5 %collective-permute-done.14.before = f32[32,8,128]{2,1,0:T(8,128)S(1)} collective-permute-done((f32[32,8,128]{2,1,0:T(8,128)S(1)}, f32[32,8,128]{2,1,0:T(8,128)S(1)}, u32[]{:S(2)}, u32[]{:S(2)}) %collective-permute-start.14) | collective-permute-done | bytes 131104 | tf_op jit(solution)/shard_map/ppermute | solution.py:279
  61.6 1.5 %shard_map.47 = (f32[32,8,128]{2,1,0:T(8,128)S(1)}, f32[4,8,8,128]{3,2,1,0:T(8,128)S(1)}) custom-call(f32[32,8,128]{2,1,0:T(8,128)S(1)} %collective-permute-done.14.before, f32[4,8,8,128]{3,2,1,0:T(8,128)S(1)} %get-tuple-element.99.kept, f32[6,32,8,128]{3,2,1,0:T(8,128)S(1)} %get-tuple-element.100.coef, f32[4,2,8,128]{3,2,1,0:T(8,128)S(1)} %get-tuple-element.101.ab), custom_call_target="tpu_custom_call" | custom-call | tf_op jit(solution)/shard_map/pallas_call | solution.py:237
  63.1 7.3 %all-gather = f32[128,8,128]{2,1,0:T(8,128)S(1)} all-gather(f32[32,8,128]{2,1,0:T(8,128)S(1)} %get-tuple-element.102), channel_id=2, replica_groups={{0,4,8,12},{16,20,24,28},{32,36,40,44},{48,52,56,60},{64,68,72,76},{80,..., dimensions={0}, use_global_device_ids=true | all-gather | bytes 655360 | tf_op jit(solution)/shard_map/all_gather | solution.py:286
  70.4 3.0 %shard_map.48 = (f32[6,2,8,128]{3,2,1,0:T(8,128)S(1)}, f32[32,8,128]{2,1,0:T(8,128)S(1)}, f32[8,8,128]{2,1,0:T(8,128)S(1)}) custom-call(f32[4,32,8,128]{3,2,1,0:T(8,128)S(1)} %bitcast.51, f32[6,32,8,128]{3,2,1,0:T(8,128)S(1)} %get-tuple-element.100.coef, f32[4,2,8,128]{3,2,1,0:T(8,128)S(1)} %get-tuple-element.101.ab), custom_call_target="tpu_custom_call" | custom-call | tf_op jit(solution)/shard_map/pallas_call | solution.py:237
  73.4 5.7 %conditional.5 = (f32[2,8,128]{2,1,0:T(8,128)S(1)}, f32[1,2,8,128]{3,2,1,0:T(8,128)S(1)}, f32[1,2,8,128]{3,2,1,0:T(8,128)S(1)}, f32[1,2,8,128]{3,2,1,0:T(8,128)S(1)}) conditional(s32[]{:T(128)} %convert_element_type.13, (f32[6,2,8,128]{3,2,1,0:T(8,128)S(1)}, s32[]{:T(128)}) %tuple.75, (s32[]{:T(128)}, f32[6,2,8,128]{3,2,1,0:T(8,128)S(1)}) %tuple.76), branch_computations={%region_0.0_spmd, %region_1.6_spmd} | conditional | flops 30729 | bytes 1335686 | solution.py:334
  73.5 1.3 %collective-permute-start.1 = (f32[4,2,8,128]{3,2,1,0:T(8,128)S(1)}, f32[4,2,8,128]{3,2,1,0:T(8,128)S(1)}, u32[]{:S(2)}, u32[]{:S(2)}) collective-permute-start(f32[4,2,8,128]{3,2,1,0:T(8,128)S(1)} %get-tuple-element.124), channel_id=1, source_target_pairs={{0,32},{4,36},{8,40},{12,44},{16,48},{20,52},{24,56},{28,60},{1,33... | collective-permute-start | bytes 98312 | tf_op jit(solution)/shard_map/cond/branch_0_fun/ppermute | solution.py:264
  74.8 0.7 collective-permute-start.3
  75.5 1.3 %collective-permute-start.2 = (f32[4,2,8,128]{3,2,1,0:T(8,128)S(1)}, f32[4,2,8,128]{3,2,1,0:T(8,128)S(1)}, u32[]{:S(2)}, u32[]{:S(2)}) collective-permute-start(f32[4,2,8,128]{3,2,1,0:T(8,128)S(1)} %get-tuple-element.126), channel_id=1, source_target_pairs={{0,16},{4,20},{8,24},{12,28},{32,48},{36,52},{40,56},{44,60},{1,17... | collective-permute-start | bytes 98312 | tf_op jit(solution)/shard_map/cond/branch_0_fun/ppermute | solution.py:264
  76.8 1.3 %collective-permute-start = (f32[4,2,8,128]{3,2,1,0:T(8,128)S(1)}, f32[4,2,8,128]{3,2,1,0:T(8,128)S(1)}, u32[]{:S(2)}, u32[]{:S(2)}) collective-permute-start(f32[4,2,8,128]{3,2,1,0:T(8,128)S(1)} %get-tuple-element.127), channel_id=1, source_target_pairs={{0,48},{4,52},{8,56},{12,60},{1,49},{5,53},{9,57},{13,61},{2,50},{... | collective-permute-start | bytes 98312 | tf_op jit(solution)/shard_map/cond/branch_0_fun/ppermute | solution.py:264
  78.1 0.0 collective-permute-done.1
  78.1 0.0 collective-permute-done.3
  78.1 0.0 collective-permute-done.2
  78.1 1.0 %collective-permute-done = f32[4,2,8,128]{3,2,1,0:T(8,128)S(1)} collective-permute-done((f32[4,2,8,128]{3,2,1,0:T(8,128)S(1)}, f32[4,2,8,128]{3,2,1,0:T(8,128)S(1)}, u32[]{:S(2)}, u32[]{:S(2)}) %collective-permute-start) | collective-permute-done | bytes 32800 | tf_op jit(solution)/shard_map/cond/branch_0_fun/ppermute | solution.py:264
  79.2 0.7 collective-permute-start.15
  79.8 0.0 collective-permute-done.15
  79.9 10.9 %all_to_all.10 = f32[16,2,2,8,128]{4,3,2,1,0:T(8,128)S(1)} all-to-all(f32[16,2,2,8,128]{4,3,2,1,0:T(8,128)S(1)} %bitcast.52), channel_id=1, replica_groups={{0,1,2,3,4,5,6,7,8,9,10,11,12,13,14,15},{16,17,18,19,20,21,22,23,24,25,..., dimensions={0} | all-to-all | bytes 524288 | tf_op jit(solution)/shard_map/all_to_all | solution.py:362
  90.8 2.6 %shard_map.50 = f32[4,8,8,128]{3,2,1,0:T(8,128)} custom-call(f32[4,4,2,2,8,128]{5,4,3,2,1,0:T(8,128)S(1)} %bitcast.53, f32[32,8,128]{2,1,0:T(8,128)S(1)} %get-tuple-element.108.prefix, f32[8,8,128]{2,1,0:T(8,128)S(1)} %get-tuple-element.109.added, f32[4,8,8,128]{3,2,1,0:T(8,128)S(1)} %get-tuple-element.110.held, ...), custom_call_target="tpu_custom_call" | custom-call | tf_op jit(solution)/shard_map/pallas_call | solution.py:237
  (9 shorter events, 0.1 us)
Async XLA Ops:
  2.0 14.9 %all-to-all-start = ((f32[4,64,8,128]{3,2,1,0:T(8,128)}), f32[4,64,8,128]{3,2,1,0:T(8,128)S(1)}, u32[]{:S(2)}, u32[]{:S(2)}) async-start(f32[4,64,8,128]{3,2,1,0:T(8,128)} %broadcast_in_dim.12), calls=%async_computation | async-start | bytes 2097152 | tf_op jit(solution)/shard_map/all_to_all | solution.py:268
  18.5 43.1 %collective-permute-start.14 = (f32[32,8,128]{2,1,0:T(8,128)S(1)}, f32[32,8,128]{2,1,0:T(8,128)S(1)}, u32[]{:S(2)}, u32[]{:S(2)}) collective-permute-start(f32[32,8,128]{2,1,0:T(8,128)S(1)} %get-tuple-element.98), channel_id=1, source_target_pairs={{0,4},{4,8},{8,12},{12,16},{16,20},{20,24},{24,28},{28,32},{32,36}... | collective-permute-start | bytes 393224 | tf_op jit(solution)/shard_map/ppermute | solution.py:279
  73.5 4.6 %collective-permute-start.1 = (f32[4,2,8,128]{3,2,1,0:T(8,128)S(1)}, f32[4,2,8,128]{3,2,1,0:T(8,128)S(1)}, u32[]{:S(2)}, u32[]{:S(2)}) collective-permute-start(f32[4,2,8,128]{3,2,1,0:T(8,128)S(1)} %get-tuple-element.124), channel_id=1, source_target_pairs={{0,32},{4,36},{8,40},{12,44},{16,48},{20,52},{24,56},{28,60},{1,33... | collective-permute-start | bytes 98312 | tf_op jit(solution)/shard_map/cond/branch_0_fun/ppermute | solution.py:264
  74.8 3.3 %collective-permute-start.3 = (f32[4,2,8,128]{3,2,1,0:T(8,128)S(1)}, f32[4,2,8,128]{3,2,1,0:T(8,128)S(1)}, u32[]{:S(2)}, u32[]{:S(2)}) collective-permute-start(f32[4,2,8,128]{3,2,1,0:T(8,128)S(1)} %get-tuple-element.125), channel_id=1, source_target_pairs={{16,32},{20,36},{24,40},{28,44},{17,33},{21,37},{25,41},{29,45},{1... | collective-permute-start | bytes 98312 | tf_op jit(solution)/shard_map/cond/branch_0_fun/ppermute | solution.py:264
  75.5 2.7 %collective-permute-start.2 = (f32[4,2,8,128]{3,2,1,0:T(8,128)S(1)}, f32[4,2,8,128]{3,2,1,0:T(8,128)S(1)}, u32[]{:S(2)}, u32[]{:S(2)}) collective-permute-start(f32[4,2,8,128]{3,2,1,0:T(8,128)S(1)} %get-tuple-element.126), channel_id=1, source_target_pairs={{0,16},{4,20},{8,24},{12,28},{32,48},{36,52},{40,56},{44,60},{1,17... | collective-permute-start | bytes 98312 | tf_op jit(solution)/shard_map/cond/branch_0_fun/ppermute | solution.py:264
  76.8 2.3 %collective-permute-start = (f32[4,2,8,128]{3,2,1,0:T(8,128)S(1)}, f32[4,2,8,128]{3,2,1,0:T(8,128)S(1)}, u32[]{:S(2)}, u32[]{:S(2)}) collective-permute-start(f32[4,2,8,128]{3,2,1,0:T(8,128)S(1)} %get-tuple-element.127), channel_id=1, source_target_pairs={{0,48},{4,52},{8,56},{12,60},{1,49},{5,53},{9,57},{13,61},{2,50},{... | collective-permute-start | bytes 98312 | tf_op jit(solution)/shard_map/cond/branch_0_fun/ppermute | solution.py:264
  79.2 0.7 collective-permute-start.15
